TPU v7x, 512 devices: a whole 4x8x8 slice. The times are simulated.
512 devices in a mesh: orb: 64 (over x, y_hi, z), tm: 8 (over y_lo, core).
Axes of the slice: x: 4, y: 8 (y_hi: 2, y_lo: 4; y = y_hi * 4 + y_lo), z: 8, core: 2. Of those that a mesh axis runs over, the one named last changes fastest.
Arguments:
- integrals: bfloat16 [8192, 128, 128], P('orb'), may hold values from -6 to 6
- block_map: int32 [512, 4], P('orb'), may hold values 0 or 1
- green_occ: bfloat16 [8, 8192, 384], P('tm', 'orb'), may hold values from -0.5 to 0.5
- green_virt: bfloat16 [8, 8192, 384], P('tm', 'orb'), may hold values from -0.5 to 0.5
- coulomb: bfloat16 [8192, 512], P('orb'), may hold values from -0.0048828125 to 0.0048828125
- cosine: float32 [8, 8], replicated, may hold values from -1 to 1
Outputs:
- spectrum: float32 [8, 8192, 512], P('tm', 'orb')
All inputs are finite; a program needn't handle non-finite values. No bound on the sum of `block_map` on one device may be relied on, other than what follows from the above.
Results may differ from a plain program's by a relative error of at most 0.0057.
Values may be sent and summed in bfloat16 or wider, within the bound.
No kernel may reach another device: no remote copies, remote signals or barrier semaphores. Data moves between devices by JAX's collectives and lax.ppermute only.
A program may use at most 128 MiB of HBM per device.

v0:
```python
import jax
import jax.numpy as jnp
from jax import lax
from jax.sharding import PartitionSpec as P


def padded(value, sides, width):
    for axis, dim in sides:
        size, length = (lax.axis_size(axis), value.shape[dim])
        up = [(i, (i + 1) % size) for i in range(size)]
        down = [(j, i) for i, j in up]
        last = lax.slice_in_dim(value, length - width, length, axis=dim)
        first = lax.slice_in_dim(value, 0, width, axis=dim)
        before = lax.ppermute(last, axis, up)
        after = lax.ppermute(first, axis, down)
        value = jnp.concatenate([before, value, after], axis=dim)
    return value


def body(integrals, block_map, green_occ, green_virt, coulomb, cosine):
    aux_rows = integrals.shape[0]
    orb_count = integrals.shape[1]
    row_blocks = block_map.shape[0]
    col_blocks = block_map.shape[1]
    pair_count = orb_count * orb_count
    keep_mask = block_map.astype(jnp.bfloat16)[:, None, :, None, None]
    shaped = integrals.reshape(
        row_blocks, aux_rows // row_blocks, col_blocks, orb_count // col_blocks, orb_count
    )
    masked = (shaped * keep_mask).reshape(aux_rows, pair_count)
    packed = jnp.concatenate([masked, coulomb], axis=1)
    groups = lax.axis_size("tm")
    row_share = aux_rows // groups
    own_slice = lax.dynamic_slice_in_dim(packed, lax.axis_index("tm") * row_share, row_share, 0)
    extended = padded(own_slice, (("orb", 0),), row_share)
    rim_pair = jnp.stack([extended[:row_share], extended[2 * row_share :]])
    whole_rims = lax.all_gather(rim_pair, "tm", axis=1, tiled=True)
    sources = [whole_rims[0], packed, whole_rims[1]]
    occ_tiles = green_occ[0].reshape(orb_count, 3, orb_count)
    virt_tiles = green_virt[0].reshape(orb_count, 3, orb_count)
    running_sum = jnp.zeros((aux_rows, coulomb.shape[1]), jnp.float32)
    for offset in range(3):
        source = sources[offset]
        other_side = source[:, :pair_count].reshape(aux_rows, orb_count, orb_count)
        other_coulomb = source[:, pair_count:]
        half_side = jnp.einsum(
            "qls,ns->qln", other_side, virt_tiles[:, offset, :], preferred_element_type=jnp.float32
        ).astype(jnp.bfloat16)
        pair_side = jnp.einsum(
            "ml,qln->qmn", occ_tiles[:, offset, :], half_side, preferred_element_type=jnp.float32
        ).astype(jnp.bfloat16)
        response = lax.dot_general(
            masked,
            pair_side.reshape(aux_rows, pair_count),
            (((1,), (1,)), ((), ())),
            preferred_element_type=jnp.float32,
        ).astype(jnp.bfloat16)
        running_sum = running_sum + jnp.dot(
            response, other_coulomb, preferred_element_type=jnp.float32
        )
    time_panel = running_sum.astype(jnp.bfloat16)
    freq_part = jnp.einsum(
        "ft,tpk->fpk",
        cosine,
        lax.all_to_all(time_panel[None], "tm", split_axis=2, concat_axis=0, tiled=True).astype(
            jnp.float32
        ),
        precision=lax.Precision.HIGHEST,
    )
    return lax.all_to_all(freq_part, "tm", split_axis=0, concat_axis=2, tiled=True)


def solution(mesh):
    in_specs = (
        P("orb", None, None),
        P("orb", None),
        P("tm", "orb", None),
        P("tm", "orb", None),
        P("orb", None),
        P(),
    )
    out_specs = P("tm", "orb", None)
    return jax.shard_map(body, mesh=mesh, in_specs=in_specs, out_specs=out_specs, check_vma=False)
```

profile of v0, /device:TPU:1, one launch (start us, length us, event | category | flops | bytes accessed | tf_op | source)
XLA Modules:
  0.0 259.0 jit_solution(831437825801169823)
XLA Ops:
  6.5 0.7 convert_element_type.43
  7.3 2.8 %mul.30 = bf16[8,16,4,32,128]{4,3,2,1,0:T(8,128)(2,1)} broadcast(bf16[8,4]{1,0:T(8,128)(2,1)S(1)} %copy.24), dimensions={0,2} | broadcast | bytes 4194368 | tf_op jit(solution)/shard_map/mul | solution.py:30
  10.2 7.4 %mul.31 = bf16[128,16384]{1,0:T(8,128)(2,1)} reshape(bf16[8,16,4,32,128]{4,3,2,1,0:T(8,128)(2,1)} %mul.30) | data formatting | bytes 8388608 | tf_op jit(solution)/shard_map/mul | solution.py:30
  17.5 6.0 %bitcast_multiply_fusion = bf16[128,16384]{1,0:T(8,128)(2,1)S(1)} fusion(bf16[128,16384]{1,0:T(8,128)(2,1)} %mul.31, bf16[16,8,128,128]{3,2,1,0:T(8,128)(2,1)} %bitcast.103), kind=kLoop, calls=%fused_computation.4 | loop fusion | flops 2097152 | bytes 12582912 | tf_op jit(solution)/shard_map/mul | solution.py:30
  23.6 5.0 %collective-permute-start = (bf16[16,16896]{1,0:T(8,128)(2,1)S(1)}, bf16[16,16896]{1,0:T(8,128)(2,1)S(1)}, u32[]{:S(2)}, u32[]{:S(2)}) collective-permute-start(bf16[16,16896]{1,0:T(8,128)(2,1)S(1)} %fusion.51), channel_id=1, source_target_pairs={{0,8},{8,16},{16,24},{24,32},{32,40},{40,48},{48,56},{56,64},{64,7... | collective-permute-start | bytes 1622024 | tf_op jit(solution)/shard_map/ppermute | solution.py:14
  28.6 16.2 %collective-permute-start.1 = (bf16[16,16896]{1,0:T(8,128)(2,1)S(1)}, bf16[16,16896]{1,0:T(8,128)(2,1)S(1)}, u32[]{:S(2)}, u32[]{:S(2)}) collective-permute-start(bf16[16,16896]{1,0:T(8,128)(2,1)S(1)} %fusion.51), channel_id=1, source_target_pairs={{8,0},{16,8},{24,16},{32,24},{40,32},{48,40},{56,48},{64,56},{72,6... | collective-permute-start | bytes 1622024 | tf_op jit(solution)/shard_map/ppermute | solution.py:15
  44.8 15.5 %collective-permute-done = bf16[16,16896]{1,0:T(8,128)(2,1)S(1)} collective-permute-done((bf16[16,16896]{1,0:T(8,128)(2,1)S(1)}, bf16[16,16896]{1,0:T(8,128)(2,1)S(1)}, u32[]{:S(2)}, u32[]{:S(2)}) %collective-permute-start) | collective-permute-done | bytes 540704 | tf_op jit(solution)/shard_map/ppermute | solution.py:14
  60.4 6.8 %collective-permute-done.1 = bf16[16,16896]{1,0:T(8,128)(2,1)S(1)} collective-permute-done((bf16[16,16896]{1,0:T(8,128)(2,1)S(1)}, bf16[16,16896]{1,0:T(8,128)(2,1)S(1)}, u32[]{:S(2)}, u32[]{:S(2)}) %collective-permute-start.1) | collective-permute-done | bytes 540704 | tf_op jit(solution)/shard_map/ppermute | solution.py:15
  67.2 1.1 pad_maximum_fusion
  68.8 5.8 %broadcast_multiply_fusion = bf16[128,128,128]{2,1,0:T(8,128)(2,1)} fusion(bf16[128,128,128]{2,1,0:T(8,128)(2,1)} %param.6, bf16[128,128]{1,0:T(8,128)(2,1)S(1)} %mul.27), kind=kLoop, calls=%fused_computation.25 | loop fusion | flops 2097152 | bytes 8421376 | tf_op jit(solution)/shard_map/mul | solution.py:30
  74.6 5.7 %convert_bitcast_fusion.1 = bf16[128,128,128]{1,2,0:T(8,128)(2,1)} fusion(bf16[128,128,128]{2,1,0:T(8,128)(2,1)} %broadcast_multiply_fusion, bf16[128,3,128]{0,2,1:T(8,128)(2,1)S(1)} %bitcast.115, bf16[128,3,128]{0,2,1:T(8,128)(2,1)S(1)} %bitcast.112), kind=kOutput, calls=%fused_computation.10 | convolution fusion | flops 1077936128 | bytes 8454144 | tf_op jit(solution)/shard_map/ml,qln->qmn/dot_general | solution.py:49
  80.4 6.8 %copy.37 = bf16[128,128,128]{2,0,1:T(8,128)(2,1)} copy(bf16[128,128,128]{1,2,0:T(8,128)(2,1)} %convert_bitcast_fusion.1) | data formatting | bytes 8388608 | tf_op jit(solution)/shard_map/convert_element_type | solution.py:51
  87.2 77.8 %all-gather.2.cloned.1.call-done = bf16[2,128,16896]{2,1,0:T(8,128)(2,1)} async-done(((bf16[2,16,16896]{2,1,0:T(8,128)(2,1)}), bf16[2,128,16896]{2,1,0:T(8,128)(2,1)}) %all-gather.2.cloned.1.call-update) | async-done | bytes 8650768 | tf_op jit(solution)/shard_map/all_gather | solution.py:37
  165.0 3.8 %slice_bitcast_fusion = (bf16[128,16896]{1,0:T(8,128)(2,1)S(1)}, bf16[128,16896]{1,0:T(8,128)(2,1)S(1)}) fusion(bf16[2,128,16896]{2,1,0:T(8,128)(2,1)} %all-gather.2.cloned.1.call-done), kind=kLoop, calls=%fused_computation | loop fusion | bytes 17301504 | tf_op jit(solution)/shard_map/squeeze | solution.py:38
  168.8 2.5 slice_bitcast_fusion.2
  171.4 0.8 copy-done.1
  172.2 1.3 copy-done.2
  173.4 3.2 %copy.52 = bf16[16,8,128,128]{3,2,1,0:T(8,128)(2,1)} copy(bf16[16,8,128,128]{3,1,2,0:T(8,128)(2,1)S(1)} %get-tuple-element.8) | data formatting | bytes 8388608
  176.7 5.8 %convert_bitcast_fusion.2 = bf16[128,128,128]{1,2,0:T(8,128)(2,1)} fusion(bf16[128,128,128]{2,1,0:T(8,128)(2,1)} %bitcast.105, bf16[128,3,128]{0,2,1:T(8,128)(2,1)S(1)} %bitcast.116, bf16[128,3,128]{0,2,1:T(8,128)(2,1)S(1)} %bitcast.113), kind=kOutput, calls=%fused_computation.13 | convolution fusion | flops 1077936128 | bytes 8454144 | tf_op jit(solution)/shard_map/ml,qln->qmn/dot_general | solution.py:49
  182.5 6.8 %copy.32 = bf16[128,128,128]{2,0,1:T(8,128)(2,1)} copy(bf16[128,128,128]{1,2,0:T(8,128)(2,1)} %convert_bitcast_fusion.2) | data formatting | bytes 8388608 | tf_op jit(solution)/shard_map/convert_element_type | solution.py:51
  189.2 6.2 %fusion.47 = f32[128,512]{1,0:T(8,128)S(1)} fusion(bf16[128,128,128]{2,0,1:T(8,128)(2,1)} %copy.32, bf16[128,128,128]{2,1,0:T(8,128)(2,1)} %broadcast_multiply_fusion, bf16[128,16896]{1,0:T(8,128)(2,1)} %copy-done.2), kind=kOutput, calls=%fused_computation.37 | convolution fusion | flops 553664512 | bytes 8781824 | tf_op jit(solution)/shard_map/dot_general | solution.py:58
  195.5 5.4 %copy.53 = bf16[16,8,128,128]{3,2,1,0:T(8,128)(2,1)} copy(bf16[16,8,128,128]{3,1,2,0:T(8,128)(2,1)} %get-tuple-element.7) | data formatting | bytes 8388608
  200.9 5.7 %convert_bitcast_fusion = bf16[128,128,128]{1,2,0:T(8,128)(2,1)} fusion(bf16[128,128,128]{2,1,0:T(8,128)(2,1)} %bitcast.104, bf16[128,3,128]{0,2,1:T(8,128)(2,1)S(1)} %bitcast.117, bf16[128,3,128]{0,2,1:T(8,128)(2,1)S(1)} %bitcast.114), kind=kOutput, calls=%fused_computation.7 | convolution fusion | flops 1077936128 | bytes 8454144 | tf_op jit(solution)/shard_map/ml,qln->qmn/dot_general | solution.py:49
  206.6 6.8 %copy.42 = bf16[128,128,128]{2,0,1:T(8,128)(2,1)} copy(bf16[128,128,128]{1,2,0:T(8,128)(2,1)} %convert_bitcast_fusion) | data formatting | bytes 8388608 | tf_op jit(solution)/shard_map/convert_element_type | solution.py:51
  213.3 6.2 %convolution_add_fusion.1 = f32[128,512]{1,0:T(8,128)S(1)} fusion(f32[128,512]{1,0:T(8,128)S(1)} %fusion.47, bf16[128,512]{1,0:T(8,128)(2,1)S(1)} %copy-done.3, bf16[128,128,128]{2,0,1:T(8,128)(2,1)} %copy.37, bf16[128,128,128]{2,1,0:T(8,128)(2,1)} %broadcast_multiply_fusion), kind=kOutput, calls=%fused_computation.27 | convolution fusion | flops 553730048 | bytes 9043968 | tf_op jit(solution)/shard_map/dot_general | solution.py:58
  219.6 6.2 %fusion.25 = bf16[1,128,512]{2,1,0:T(8,128)(2,1)S(1)} fusion(f32[128,512]{1,0:T(8,128)S(1)} %convolution_add_fusion.1, bf16[128,128,128]{2,0,1:T(8,128)(2,1)} %copy.42, bf16[128,128,128]{2,1,0:T(8,128)(2,1)} %broadcast_multiply_fusion, bf16[128,16896]{1,0:T(8,128)(2,1)} %copy-done.1), kind=kOutput, calls=%fused_computation.30 | convolution fusion | flops 553795584 | bytes 8912896 | tf_op jit(solution)/shard_map/dot_general | solution.py:58
  226.0 0.5 broadcast.10
  226.5 1.4 reduce
  228.0 10.6 %all_to_all.36 = bf16[8,2,4096]{2,1,0:T(2,128)(2,1)S(1)} all-to-all(bf16[8,2,4096]{2,1,0:T(2,128)(2,1)S(1)} %reshape.39), channel_id=1, replica_groups=mesh['orb'=64,'tm'=8] {'tm'}, dimensions={0} | all-to-all | bytes 262144 | tf_op jit(solution)/shard_map/all_to_all | solution.py:65
  238.8 0.3 convolution_bitcast_fusion
  239.1 12.1 %all_to_all.37 = f32[8,128,64]{1,2,0:T(8,128)S(1)} all-to-all(f32[8,128,64]{1,2,0:T(8,128)S(1)} %copy.45), channel_id=1, replica_groups=mesh['orb'=64,'tm'=8] {'tm'}, dimensions={0} | all-to-all | bytes 524288 | tf_op jit(solution)/shard_map/all_to_all | solution.py:70
  251.3 0.8 copy.46
  (23 shorter events, 1.1 us)
Async XLA Ops:
  6.5 232.2 %copy-start = (f32[8,8]{1,0:T(8,128)S(1)}, f32[8,8]{1,0:T(8,128)}, u32[]{:S(2)}) copy-start(f32[8,8]{1,0:T(8,128)} %param.11) | copy-start | bytes 772
  6.5 158.4 %all-gather.2.cloned.1.call-start = ((), (), s32[]{:S(2)}) async-start(), calls=%async_computation.2 | async-start | bytes 9732096 | tf_op jit(solution)/shard_map/all_gather | solution.py:37
  17.5 6.0 %copy-start.3 = (bf16[128,512]{1,0:T(8,128)(2,1)S(1)}, bf16[128,512]{1,0:T(8,128)(2,1)}, u32[]{:S(2)}) copy-start(bf16[128,512]{1,0:T(8,128)(2,1)} %param.10) | copy-start | bytes 393220
  23.6 44.7 %copy-start.4 = (bf16[1,128,384]{2,1,0:T(8,128)(2,1)S(1)}, bf16[1,128,384]{2,1,0:T(8,128)(2,1)}, u32[]{:S(2)}) copy-start(bf16[1,128,384]{2,1,0:T(8,128)(2,1)} %param.9) | copy-start | bytes 294916
  23.6 44.9 %copy-start.5 = (bf16[1,128,384]{2,1,0:T(8,128)(2,1)S(1)}, bf16[1,128,384]{2,1,0:T(8,128)(2,1)}, u32[]{:S(2)}) copy-start(bf16[1,128,384]{2,1,0:T(8,128)(2,1)} %param.8) | copy-start | bytes 294916
  23.6 36.7 %collective-permute-start = (bf16[16,16896]{1,0:T(8,128)(2,1)S(1)}, bf16[16,16896]{1,0:T(8,128)(2,1)S(1)}, u32[]{:S(2)}, u32[]{:S(2)}) collective-permute-start(bf16[16,16896]{1,0:T(8,128)(2,1)S(1)} %fusion.51), channel_id=1, source_target_pairs={{0,8},{8,16},{16,24},{24,32},{32,40},{40,48},{48,56},{56,64},{64,7... | collective-permute-start | bytes 1622024 | tf_op jit(solution)/shard_map/ppermute | solution.py:14
  28.6 38.6 %collective-permute-start.1 = (bf16[16,16896]{1,0:T(8,128)(2,1)S(1)}, bf16[16,16896]{1,0:T(8,128)(2,1)S(1)}, u32[]{:S(2)}, u32[]{:S(2)}) collective-permute-start(bf16[16,16896]{1,0:T(8,128)(2,1)S(1)} %fusion.51), channel_id=1, source_target_pairs={{8,0},{16,8},{24,16},{32,24},{40,32},{48,40},{56,48},{64,56},{72,6... | collective-permute-start | bytes 1622024 | tf_op jit(solution)/shard_map/ppermute | solution.py:15
  168.8 3.3 %copy-start.1 = (bf16[128,16896]{1,0:T(8,128)(2,1)}, bf16[128,16896]{1,0:T(8,128)(2,1)S(1)}, u32[]{:S(2)}) copy-start(bf16[128,16896]{1,0:T(8,128)(2,1)S(1)} %get-tuple-element.5) | copy-start | bytes 12976132
  168.8 4.6 %copy-start.2 = (bf16[128,16896]{1,0:T(8,128)(2,1)}, bf16[128,16896]{1,0:T(8,128)(2,1)S(1)}, u32[]{:S(2)}) copy-start(bf16[128,16896]{1,0:T(8,128)(2,1)S(1)} %get-tuple-element.6) | copy-start | bytes 12976132
Sparse Core Ops, SparseCore 0:
  68.4 96.5 all-gather.1
where the time goes:
time: 260 us; the launch traced here: 259 us
  waiting for transfers between devices  100 us (38%)
  local copies, waits for them, and re-layouts  50 us (19%)
  matrix products  36.2 us (14%)
  blocking collectives  22.8 us (9%)
  starting transfers between devices  21.2 us (8%)
  other arithmetic  15.1 us (6%)
  between operations  13.6 us (5%)
    all_gather x1, waiting for transfers between devices, body(): whole_rims = lax.all_gather(rim_pair, 'tm', axis=1, tiled=True)  77.8 us
    convert_element_type x3, local copies, waits for them, and re-layouts, body(): pair_side = jnp.einsum('ml,qln->qmn', occ_tiles[:, offset, :], half_side,...  20.3 us
    dot_general x3, matrix products, body(): jnp.dot(response, other_coulomb, preferred_element_type=jnp.float32)  18.7 us
    dot_general x3, matrix products, body(): jnp.einsum('ml,qln->qmn', occ_tiles[:, offset, :], half_side, preferred_e...  17.2 us
    ppermute x1, starting transfers between devices, padded(): after = lax.ppermute(first, axis, down)  16.2 us
    ppermute x1, waiting for transfers between devices, padded(): before = lax.ppermute(last, axis, up)  15.5 us
    unnamed x21, local copies, waits for them, and re-layouts  14.2 us
    all_to_all x1, blocking collectives, body(): lax.all_to_all(freq_part, 'tm', split_axis=0, concat_axis=2, tiled=True)  12.1 us
  transfers between devices with their start and end apart: 3, of which 3 were waited for; matrix products, arithmetic and copies ran while one was open for 7% of the time, Pallas kernels for 0%

commit v1 on v0

v1 whole, which is shorter than its diff:
```python
import functools

import jax
import jax.numpy as jnp
from jax import lax
from jax.experimental import pallas as pl
from jax.experimental.pallas import tpu as pltpu
from jax.sharding import PartitionSpec as P

NT = (((1,), (1,)), ((), ()))
VMEM = pl.BlockSpec(memory_space=pltpu.VMEM)


def flatten_kernel(source, out, wide):
    count, orb, _ = source.shape
    pitch = wide.shape[0] // count
    for p in range(count):
        wide[p * pitch : p * pitch + orb, :] = source[p].astype(jnp.float32)
    for m in range(orb):
        out[:, m * orb : (m + 1) * orb] = wide[pl.ds(m, count, stride=pitch), :].astype(out.dtype)


def flatten(integrals):
    count, orb, _ = integrals.shape
    width = count // 2
    return pl.pallas_call(
        flatten_kernel,
        out_shape=jax.ShapeDtypeStruct((count, orb * orb), integrals.dtype),
        grid=(count // width,),
        in_specs=[pl.BlockSpec((width, orb, orb), lambda i: (i, 0, 0))],
        out_specs=pl.BlockSpec((width, orb * orb), lambda i: (i, 0)),
        scratch_shapes=[pltpu.VMEM((width * (orb + 8), orb), jnp.float32)],
        name="flat",
    )(integrals)


def share_kernel(nq, nt, orb, count, select, *refs):
    sources = refs[:count]
    occ, virt, own_far, keep, weights = refs[count : count + 5]
    outs = refs[count + 5 : 2 * count + 5]
    half, pair, own, arrived = refs[2 * count + 5 :]
    fetch = pltpu.make_async_copy(own_far, own, arrived)
    fetch.start()
    rows = nq * nt * count
    pitch = pair.shape[0] // rows
    group = min(nq, 4)

    for k in range(count):
        lane0 = pl.ds(pl.multiple_of(select[k] * orb, orb), orb)

        def half_step(i, carry):
            tiles = virt[pl.ds(2 * i, 2), :, lane0].reshape(2 * orb, orb)
            for g in range(nq // group):
                left = sources[k][g * group : (g + 1) * group].reshape(group * orb, orb)
                value = lax.dot_general(left, tiles, NT, preferred_element_type=jnp.float32)
                half[g * group : (g + 1) * group, :, pl.ds(pl.multiple_of(2 * i * orb, 2 * orb), 2 * orb)] = (
                    value.astype(jnp.bfloat16).reshape(group, orb, 2 * orb)
                )
            return carry

        lax.fori_loop(0, nt // 2, half_step, 0, unroll=True)

        def pair_step(t, carry):
            tile = occ[t, :, lane0]
            lanes = pl.ds(pl.multiple_of(t * orb, orb), orb)
            for q in range(0, nq, 2):
                right = jnp.concatenate([half[q, :, lanes], half[q + 1, :, lanes]], axis=1)
                value = jnp.dot(tile, right, preferred_element_type=jnp.float32)
                row = pl.multiple_of(((k * nt + t) * nq + q) * pitch, 8)
                pair[pl.ds(row, orb), :] = value[:, :orb]
                pair[pl.ds(row + pitch, orb), :] = value[:, orb:]
            return carry

        lax.fori_loop(0, nt, pair_step, 0, unroll=4)

    fetch.wait()
    blocks = keep.shape[0]
    chunk = orb // blocks

    def response_step(c, total):
        left = jnp.concatenate(
            [pair[pl.ds(c * chunk + i, rows, stride=pitch), :].astype(jnp.bfloat16) for i in range(chunk)],
            axis=1,
        )
        right = own[:, pl.ds(pl.multiple_of(c * chunk * orb, chunk * orb), chunk * orb)]
        value = lax.dot_general(left, right, NT, preferred_element_type=jnp.float32)
        return total + value * keep[c]

    total = lax.fori_loop(0, blocks, response_step, jnp.zeros((rows, own.shape[0]), jnp.float32))
    response = total.astype(jnp.bfloat16)
    for k in range(count):
        piece = response[k * nq * nt : (k + 1) * nq * nt]
        result = jnp.dot(weights[0], piece, preferred_element_type=jnp.float32)
        for i in range(1, weights.shape[0]):
            result += jnp.dot(weights[i], piece, preferred_element_type=jnp.float32)
        outs[k][...] = result.astype(outs[k].dtype)


def share_call(select, sources, occ, virt, own, keep, weights):
    nq, orb, _ = sources[0].shape
    nt = occ.shape[0]
    count = len(sources)
    pitch = orb + 8
    out = jax.ShapeDtypeStruct((weights.shape[1], own.shape[0]), jnp.bfloat16)
    return pl.pallas_call(
        functools.partial(share_kernel, nq, nt, orb, count),
        out_shape=[out] * count,
        in_specs=[pl.BlockSpec(memory_space=pltpu.SMEM)]
        + [VMEM] * (count + 2)
        + [pl.BlockSpec(memory_space=pltpu.HBM)]
        + [VMEM] * 2,
        out_specs=[VMEM] * count,
        scratch_shapes=[
            pltpu.VMEM((nq, orb, nt * orb), jnp.bfloat16),
            pltpu.VMEM((nq * nt * count * pitch, orb), jnp.float32),
            pltpu.VMEM(own.shape, own.dtype),
            pltpu.SemaphoreType.DMA,
        ],
        compiler_params=pltpu.CompilerParams(vmem_limit_bytes=40 * 2**20),
    )(select, *sources, occ, virt, own, keep, weights)


AXES = ("orb", "tm")
SEGMENT = 8


def chain_pairs(domains, groups, first, step):
    pairs = []
    for here in range(first, domains, 2):
        there = (here + step) % domains
        far = here // SEGMENT != there // SEGMENT
        for t in range(groups):
            pairs.append((here * groups + t, there * groups + (mirrored(groups, t) if far else t)))
    return pairs


def mirrored(groups, t):
    return groups - 2 - t + 2 * (t % 2)


def cosine_weights(cosine, nq):
    full = (cosine[:, None, :, None] * jnp.eye(nq, dtype=jnp.float32)[None, :, None, :]).reshape(
        cosine.shape[0] * nq, cosine.shape[1] * nq
    )
    terms = []
    for _ in range(3):
        term = lax.reduce_precision(full, 8, 7)
        terms.append(term.astype(jnp.bfloat16))
        full = full - term
    return jnp.stack(terms)


def tie(value, *others):
    return lax.optimization_barrier((value,) + others)[0]


def body(integrals, block_map, green_occ, green_virt, coulomb, cosine):
    return steps(integrals, block_map, green_occ[0], green_virt[0], coulomb, cosine)


def steps(integrals, block_map, occ_own, virt_own, coulomb, cosine):
    aux_rows, orb, _ = integrals.shape
    row_blocks, col_blocks = block_map.shape
    groups = lax.axis_size("tm")
    domains = lax.axis_size("orb")
    share = aux_rows // groups
    here = lax.axis_index("orb")
    t = lax.axis_index("tm")
    core = t % 2
    odd = here % 2
    place = here % SEGMENT
    far = (place == 0) | (place == SEGMENT - 1)
    map_rows = jnp.repeat(block_map, aux_rows // row_blocks, axis=0)

    def cut(index):
        rows = lax.dynamic_slice_in_dim(integrals, index * share, share, 0)
        mask = lax.dynamic_slice_in_dim(map_rows, index * share, share, 0).astype(jnp.bfloat16)
        return rows * jnp.repeat(mask, orb // col_blocks, axis=1)[:, :, None]

    far_pairs = chain_pairs(domains, groups, 1, 1) + chain_pairs(domains, groups, 0, -1)
    even = chain_pairs(domains, groups, 0, 1) + chain_pairs(domains, groups, 1, -1)
    twin = [(i, i ^ 1) for i in range(groups)]
    far_share = cut(jnp.where(far, mirrored(groups, t), t))
    own_share = cut(tie(t, far_share))
    give = jnp.where(core == 0, virt_own, occ_own)
    kept = jnp.where(core == 0, occ_own, virt_own)
    got = lax.ppermute(give, "tm", twin)
    both = jnp.where(core == 0, jnp.stack([kept, got]), jnp.stack([got, kept]))
    lines = [list(range(c, groups, 2)) for c in range(2)]
    spread = jnp.broadcast_to(both[None], (groups // 2,) + both.shape)
    mine = lax.all_to_all(
        spread, "tm", split_axis=0, concat_axis=0, tiled=True, axis_index_groups=lines
    ).reshape(groups, orb, -1)
    source_b = lax.ppermute(far_share, AXES, far_pairs)
    source_a = lax.ppermute(own_share, AXES, even)
    coulomb_b = lax.ppermute(coulomb, AXES, far_pairs)
    coulomb_a = lax.ppermute(coulomb, AXES, even)
    own = flatten(integrals)
    other = lax.ppermute(mine, "tm", twin)
    occ = jnp.where(core == 0, mine, other)
    virt = jnp.where(core == 0, other, mine)
    keep = jnp.repeat(block_map.T.astype(jnp.float32), aux_rows // row_blocks, axis=1)[:, None, :]
    weights = cosine_weights(cosine, share)
    near = jnp.stack([1 + 0 * odd, 2 - 2 * odd]).astype(jnp.int32)
    part_own, part_a = share_call(near, (own_share, source_a), occ, virt, own, keep, weights)
    (part_b,) = share_call(
        (2 * odd).astype(jnp.int32)[None], (source_b,), occ, virt, own, keep, weights
    )
    mixed = jnp.concatenate([x.reshape(groups, share, aux_rows) for x in (part_own, part_a, part_b)], axis=1)
    mixed = lax.all_to_all(mixed, "tm", split_axis=0, concat_axis=0, tiled=True)
    columns = jnp.concatenate(
        [c.reshape(groups, share, c.shape[1]) for c in (coulomb, coulomb_a, coulomb_b)], axis=1
    )
    return lax.dot_general(
        mixed.reshape(-1, aux_rows),
        columns.reshape(-1, coulomb.shape[1]),
        (((0,), (0,)), ((), ())),
        preferred_element_type=jnp.float32,
    )[None]


def solution(mesh):
    in_specs = (
        P("orb", None, None),
        P("orb", None),
        P("tm", "orb", None),
        P("tm", "orb", None),
        P("orb", None),
        P(),
    )
    out_specs = P("tm", "orb", None)
    return jax.shard_map(body, mesh=mesh, in_specs=in_specs, out_specs=out_specs, check_vma=False)
```

time: 260 us -> 94 us (0.36)
  waiting for transfers between devices: 100 us -> 14.9 us
  local copies, waits for them, and re-layouts: 50 us -> 4.61 us
  matrix products: 36.2 us -> 0.96 us
  starting transfers between devices: 21.2 us -> 46.5 us
  blocking collectives: 22.8 us -> 0 us
  Pallas kernels: 0 us -> 20.3 us
  between operations: 13.6 us -> 0.25 us
  other arithmetic: 15.1 us -> 5.92 us
    all_gather x1 -> x0, waiting for transfers between devices: 77.8 us -> none  [body(): whole_rims = lax.all_gather(rim_pair, 'tm', axis=1, tiled=True)]
    dot_general x7 -> x1, matrix products: 36.2 us -> 0.96 us  [steps(): lax.dot_general(mixed.reshape(-1, aux_rows), columns.reshape(-1, coulomb....]
    all_to_all x2 -> x0, blocking collectives: 22.8 us -> none  [the longest x1 12.1 us: body(): lax.all_to_all(freq_part, 'tm', split_axis=0, concat_axis=2, tiled=True)]
    convert_element_type x4 -> x0, local copies, waits for them, and re-layouts: 20.4 us -> none  [the longest x3 20.3 us: body(): pair_side = jnp.einsum('ml,qln->qmn', occ_tiles[:, offset, :], half_side,...]
    pallas_call x0 -> x3, Pallas kernels: none -> 20.3 us  [the longest x2 15.2 us: share_call(): pl.pallas_call(functools.partial(share_kernel, nq, nt, orb, count), out_s...]
    ppermute x2 -> x6, starting transfers between devices: 21.2 us -> 38.6 us  [the longest x1 13 us: steps(): source_b = lax.ppermute(far_share, AXES, far_pairs)]
    unnamed x21 -> x9, local copies, waits for them, and re-layouts: 14.2 us -> 2.97 us
    mul x4 -> x3, local copies, waits for them, and re-layouts: 10.4 us -> 0.36 us  [the longest x1 0.19 us: cosine_weights(): cosine[:, None, :, None] * jnp.eye(nq, dtype=jnp.float32)[None, :, None, :]]
  transfers between devices with their start and end apart: 3 -> 8, of which waited for: 3 -> 4; matrix products, arithmetic and copies ran while one was open for 7% -> 6% of each run, Pallas kernels for 0% -> 11%
where the time goes in v1:
time: 94 us; the launch traced here: 93.4 us
  starting transfers between devices  46.5 us (49%)
  Pallas kernels  20.3 us (22%)
  waiting for transfers between devices  14.9 us (16%)
  other arithmetic  5.92 us (6%)
  local copies, waits for them, and re-layouts  4.61 us (5%)
  matrix products  0.96 us (1%)
    pallas_call x2, Pallas kernels, share_call(): pl.pallas_call(functools.partial(share_kernel, nq, nt, orb, count), out_s...  15.2 us
    ppermute x1, starting transfers between devices, steps(): source_b = lax.ppermute(far_share, AXES, far_pairs)  13 us
    ppermute x1, starting transfers between devices, steps(): coulomb_b = lax.ppermute(coulomb, AXES, far_pairs)  10.2 us
    ppermute x1, starting transfers between devices, steps(): got = lax.ppermute(give, 'tm', twin)  8.75 us
    ppermute x1, waiting for transfers between devices, steps(): source_b = lax.ppermute(far_share, AXES, far_pairs)  8.03 us
    pallas_call x1, Pallas kernels, flatten(): pl.pallas_call(flatten_kernel, out_shape=jax.ShapeDtypeStruct((count, orb...  5.09 us
    all_to_all x1, starting transfers between devices, steps(): mixed = lax.all_to_all(mixed, 'tm', split_axis=0, concat_axis=0, tiled=True)  4.39 us
    ppermute x1, waiting for transfers between devices, steps(): coulomb_b = lax.ppermute(coulomb, AXES, far_pairs)  4.36 us
  transfers between devices with their start and end apart: 8, of which 4 were waited for; matrix products, arithmetic and copies ran while one was open for 6% of the time, Pallas kernels for 11%

profile of v1, /device:TPU:1, one launch (start us, length us, event | category | flops | bytes accessed | tf_op | source)
XLA Modules:
  0.0 93.4 jit_solution(6608358459011645698)
XLA Ops:
  0.0 1.0 %broadcast_select_fusion.2 = (bf16[1,128,384]{2,1,0:T(8,128)(2,1)S(1)}, bf16[128,384]{1,0:T(8,128)(2,1)S(1)}) fusion(bf16[1,128,384]{2,1,0:T(8,128)(2,1)} %param.8, bf16[1,128,384]{2,1,0:T(8,128)(2,1)} %param.9, pred[]{:T(512)S(6)} %eq.27), kind=kLoop, calls=%fused_computation.15 | loop fusion | flops 98304 | bytes 393217 | tf_op jit(solution)/shard_map/jit(_where)/select_n | solution.py:186
  1.0 8.7 %collective-permute-start.1 = (bf16[128,384]{1,0:T(8,128)(2,1)S(1)}, bf16[128,384]{1,0:T(8,128)(2,1)S(1)}, u32[]{:S(2)}, u32[]{:S(2)}) collective-permute-start(bf16[128,384]{1,0:T(8,128)(2,1)S(1)} %get-tuple-element.14), channel_id=1, source_target_pairs={{0,1},{1,0},{2,3},{3,2},{4,5},{5,4},{6,7},{7,6},{8,9},{9,8},{10,11... | collective-permute-start | bytes 294920 | tf_op jit(solution)/shard_map/ppermute | solution.py:187
  9.7 0.9 collective-permute-done.1
  10.7 1.0 %broadcast_in_dim.29 = bf16[4,2,128,384]{3,2,1,0:T(8,128)(2,1)} broadcast(bf16[2,128,384]{2,1,0:T(8,128)(2,1)S(1)} %maximum_select_fusion), dimensions={1,2,3} | broadcast | bytes 983040 | tf_op jit(solution)/shard_map/broadcast_in_dim | solution.py:190
  11.6 3.5 %all-to-all-start = ((bf16[4,2,128,384]{3,2,1,0:T(8,128)(2,1)}), bf16[4,2,128,384]{3,2,1,0:T(8,128)(2,1)S(1)}, u32[]{:S(2)}, u32[]{:S(2)}) async-start(bf16[4,2,128,384]{3,2,1,0:T(8,128)(2,1)} %broadcast_in_dim.29), calls=%async_computation | async-start | bytes 1572864 | tf_op jit(solution)/shard_map/all_to_all | solution.py:191
  15.2 0.8 copy.7
  15.9 0.1 broadcast_in_dim.27
  16.0 0.1 mul.70
  16.1 1.4 %dynamic-slice_multiply_fusion.1 = bf16[16,128,128]{2,1,0:T(8,128)(2,1)S(1)} fusion(bf16[128,128,128]{2,1,0:T(8,128)(2,1)} %source.1, s32[]{:T(128)S(6)} %select_n.72, bf16[16,128]{1,0:T(8,128)(2,1)S(1)} %mul.70), kind=kLoop, calls=%fused_computation.4 | loop fusion | flops 262144 | bytes 1052676 | tf_op jit(solution)/shard_map/mul | solution.py:178
  17.5 13.0 %collective-permute-start.3 = (bf16[16,128,128]{2,1,0:T(8,128)(2,1)S(1)}, bf16[16,128,128]{2,1,0:T(8,128)(2,1)S(1)}, u32[]{:S(2)}, u32[]{:S(2)}) collective-permute-start(bf16[16,128,128]{2,1,0:T(8,128)(2,1)S(1)} %dynamic-slice_multiply_fusion.1), channel_id=1, source_target_pairs={{8,16},{9,17},{10,18},{11,19},{12,20},{13,21},{14,22},{15,23},{24,... | collective-permute-start | bytes 1572872 | tf_op jit(solution)/shard_map/ppermute | solution.py:194
  30.5 0.1 broadcast_in_dim.28
  30.6 0.1 mul.74
  30.7 1.4 %dynamic-slice_multiply_fusion.refs_0_ = bf16[16,128,128]{2,1,0:T(8,128)(2,1)S(1)} fusion(bf16[128,128,128]{2,1,0:T(8,128)(2,1)} %source.1, s32[]{:T(128)S(6)} %select_n.73, bf16[16,128]{1,0:T(8,128)(2,1)S(1)} %mul.74), kind=kLoop, calls=%fused_computation.3 | loop fusion | flops 262144 | bytes 1052676 | tf_op jit(solution)/shard_map/mul | solution.py:178
  32.1 1.9 %collective-permute-start = (bf16[16,128,128]{2,1,0:T(8,128)(2,1)S(1)}, bf16[16,128,128]{2,1,0:T(8,128)(2,1)S(1)}, u32[]{:S(2)}, u32[]{:S(2)}) collective-permute-start(bf16[16,128,128]{2,1,0:T(8,128)(2,1)S(1)} %dynamic-slice_multiply_fusion.refs_0_), channel_id=1, source_target_pairs={{0,8},{1,9},{2,10},{3,11},{4,12},{5,13},{6,14},{7,15},{16,24},{17,... | collective-permute-start | bytes 1572872 | tf_op jit(solution)/shard_map/ppermute | solution.py:195
  34.0 5.1 %flat.1.refs_4_.refs_3_ = bf16[128,16384]{1,0:T(8,128)(2,1)} custom-call(bf16[128,128,128]{2,1,0:T(8,128)(2,1)} %source.1), custom_call_target="tpu_custom_call" | custom-call | tf_op jit(solution)/shard_map/flat/pallas_call | solution.py:26
  39.2 0.1 broadcast_in_dim_reshape.2.refs_5_.refs_4_
  39.3 2.8 %collective-permute-start.2 = (bf16[8,128,384]{2,1,0:T(8,128)(2,1)S(1)}, bf16[8,128,384]{2,1,0:T(8,128)(2,1)}, u32[]{:S(2)}, u32[]{:S(2)}) collective-permute-start(bf16[8,128,384]{2,1,0:T(8,128)(2,1)S(1)} %bitcast.26), channel_id=1, source_target_pairs={{0,1},{1,0},{2,3},{3,2},{4,5},{5,4},{6,7},{7,6},{8,9},{9,8},{10,11... | collective-permute-start | bytes 2359304 | tf_op jit(solution)/shard_map/ppermute | solution.py:199
  42.2 0.1 broadcast_multiply_fusion
  42.3 0.2 mul.80
  42.5 0.1 pad_add_fusion.select
  42.6 1.6 %collective-permute-done.2 = bf16[8,128,384]{2,1,0:T(8,128)(2,1)} collective-permute-done((bf16[8,128,384]{2,1,0:T(8,128)(2,1)S(1)}, bf16[8,128,384]{2,1,0:T(8,128)(2,1)}, u32[]{:S(2)}, u32[]{:S(2)}) %collective-permute-start.2) | collective-permute-done | bytes 786464 | tf_op jit(solution)/shard_map/ppermute | solution.py:199
  44.2 1.3 %broadcast_select_fusion = (bf16[8,128,384]{2,1,0:T(8,128)(2,1)S(1)}, bf16[8,128,384]{2,1,0:T(8,128)(2,1)S(1)}) fusion(bf16[8,128,384]{2,1,0:T(8,128)(2,1)} %collective-permute-done.2, pred[]{:T(512)S(6)} %eq.27, bf16[4,2,128,384]{3,2,1,0:T(8,128)(2,1)S(1)} %all-to-all-done), kind=kLoop, calls=%fused_computation.1 | loop fusion | flops 786432 | bytes 3145729 | tf_op jit(solution)/shard_map/jit(_where)/select_n | solution.py:201
  45.4 8.0 %collective-permute-done.3.refs_0_ = bf16[16,128,128]{2,1,0:T(8,128)(2,1)S(1)} collective-permute-done((bf16[16,128,128]{2,1,0:T(8,128)(2,1)S(1)}, bf16[16,128,128]{2,1,0:T(8,128)(2,1)S(1)}, u32[]{:S(2)}, u32[]{:S(2)}) %collective-permute-start.3) | collective-permute-done | bytes 524320 | tf_op jit(solution)/shard_map/ppermute | solution.py:194
  53.5 2.2 %copy-done = bf16[128,16384]{1,0:T(8,128)(2,1)S(1)} copy-done((bf16[128,16384]{1,0:T(8,128)(2,1)S(1)}, bf16[128,16384]{1,0:T(8,128)(2,1)}, u32[]{:S(2)}) %copy-start) | copy-done | bytes 4194328
  55.7 5.4 %shard_map.65 = bf16[128,128]{1,0:T(8,128)(2,1)S(1)} custom-call(s32[1]{0:T(128)} %bitcast.8.select, bf16[16,128,128]{2,1,0:T(8,128)(2,1)S(1)} %collective-permute-done.3.refs_0_, bf16[8,128,384]{2,1,0:T(8,128)(2,1)S(1)} %get-tuple-element.12.refs_2_.refs_1_, bf16[8,128,384]{2,1,0:T(8,128)(2,1)S(1)} %get-tuple-element.11.refs_3_.refs_2_, ...), custom_call_target="tpu_custom_call" | custom-call | tf_op jit(solution)/shard_map/pallas_call | solution.py:105
  61.1 9.8 %shard_map.64 = (bf16[128,128]{1,0:T(8,128)(2,1)S(1)}, bf16[128,128]{1,0:T(8,128)(2,1)S(1)}) custom-call(s32[2]{0:T(128)S(1)} %pad_add_fusion.select, bf16[16,128,128]{2,1,0:T(8,128)(2,1)S(1)} %dynamic-slice_multiply_fusion.refs_0_, bf16[16,128,128]{2,1,0:T(8,128)(2,1)S(1)} %collective-permute-done.refs_1_, ...), custom_call_target="tpu_custom_call" | custom-call | tf_op jit(solution)/shard_map/pallas_call | solution.py:105
  70.9 0.6 pad_maximum_fusion.1
  71.5 4.4 %all-to-all-start.1 = ((bf16[8,48,128]{2,1,0:T(8,128)(2,1)}), bf16[8,48,128]{2,1,0:T(8,128)(2,1)S(1)}, u32[]{:S(2)}, u32[]{:S(2)}) async-start(bf16[8,48,128]{2,1,0:T(8,128)(2,1)} %pad_maximum_fusion.1), calls=%async_computation.1 | async-start | bytes 196608 | tf_op jit(solution)/shard_map/all_to_all | solution.py:210
  75.9 10.2 %collective-permute-start.5 = (bf16[128,512]{1,0:T(8,128)(2,1)S(1)}, bf16[128,512]{1,0:T(8,128)(2,1)S(1)}, u32[]{:S(2)}, u32[]{:S(2)}) collective-permute-start(bf16[128,512]{1,0:T(8,128)(2,1)S(1)} %copy-done.3), channel_id=1, source_target_pairs={{8,16},{9,17},{10,18},{11,19},{12,20},{13,21},{14,22},{15,23},{24,... | collective-permute-start | bytes 393224 | tf_op jit(solution)/shard_map/ppermute | solution.py:196
  86.2 1.9 %collective-permute-start.4 = (bf16[128,512]{1,0:T(8,128)(2,1)S(1)}, bf16[128,512]{1,0:T(8,128)(2,1)S(1)}, u32[]{:S(2)}, u32[]{:S(2)}) collective-permute-start(bf16[128,512]{1,0:T(8,128)(2,1)S(1)} %copy-done.3), channel_id=1, source_target_pairs={{0,8},{1,9},{2,10},{3,11},{4,12},{5,13},{6,14},{7,15},{16,24},{17,... | collective-permute-start | bytes 393224 | tf_op jit(solution)/shard_map/ppermute | solution.py:197
  88.1 4.4 %collective-permute-done.5 = bf16[128,512]{1,0:T(8,128)(2,1)S(1)} collective-permute-done((bf16[128,512]{1,0:T(8,128)(2,1)S(1)}, bf16[128,512]{1,0:T(8,128)(2,1)S(1)}, u32[]{:S(2)}, u32[]{:S(2)}) %collective-permute-start.5) | collective-permute-done | bytes 131104 | tf_op jit(solution)/shard_map/ppermute | solution.py:196
  92.5 1.0 %convolution_bitcast_fusion = f32[1,128,512]{2,1,0:T(8,128)} fusion(bf16[8,48,128]{2,1,0:T(8,128)(2,1)S(1)} %all-to-all-done.1, bf16[8,16,512]{2,1,0:T(8,128)(2,1)S(1)} %bitcast.31, bf16[8,16,512]{2,1,0:T(8,128)(2,1)S(1)} %bitcast.32, bf16[8,16,512]{2,1,0:T(8,128)(2,1)S(1)} %bitcast.30), kind=kOutput, calls=%fused_computation | convolution fusion | flops 51511296 | bytes 753664 | tf_op jit(solution)/shard_map/dot_general | solution.py:214
  (20 shorter events, 0.2 us)
Async XLA Ops:
  1.0 9.7 %collective-permute-start.1 = (bf16[128,384]{1,0:T(8,128)(2,1)S(1)}, bf16[128,384]{1,0:T(8,128)(2,1)S(1)}, u32[]{:S(2)}, u32[]{:S(2)}) collective-permute-start(bf16[128,384]{1,0:T(8,128)(2,1)S(1)} %get-tuple-element.14), channel_id=1, source_target_pairs={{0,1},{1,0},{2,3},{3,2},{4,5},{5,4},{6,7},{7,6},{8,9},{9,8},{10,11... | collective-permute-start | bytes 294920 | tf_op jit(solution)/shard_map/ppermute | solution.py:187
  11.6 27.7 %all-to-all-start = ((bf16[4,2,128,384]{3,2,1,0:T(8,128)(2,1)}), bf16[4,2,128,384]{3,2,1,0:T(8,128)(2,1)S(1)}, u32[]{:S(2)}, u32[]{:S(2)}) async-start(bf16[4,2,128,384]{3,2,1,0:T(8,128)(2,1)} %broadcast_in_dim.29), calls=%async_computation | async-start | bytes 1572864 | tf_op jit(solution)/shard_map/all_to_all | solution.py:191
  17.5 36.0 %collective-permute-start.3 = (bf16[16,128,128]{2,1,0:T(8,128)(2,1)S(1)}, bf16[16,128,128]{2,1,0:T(8,128)(2,1)S(1)}, u32[]{:S(2)}, u32[]{:S(2)}) collective-permute-start(bf16[16,128,128]{2,1,0:T(8,128)(2,1)S(1)} %dynamic-slice_multiply_fusion.1), channel_id=1, source_target_pairs={{8,16},{9,17},{10,18},{11,19},{12,20},{13,21},{14,22},{15,23},{24,... | collective-permute-start | bytes 1572872 | tf_op jit(solution)/shard_map/ppermute | solution.py:194
  32.1 29.0 %collective-permute-start = (bf16[16,128,128]{2,1,0:T(8,128)(2,1)S(1)}, bf16[16,128,128]{2,1,0:T(8,128)(2,1)S(1)}, u32[]{:S(2)}, u32[]{:S(2)}) collective-permute-start(bf16[16,128,128]{2,1,0:T(8,128)(2,1)S(1)} %dynamic-slice_multiply_fusion.refs_0_), channel_id=1, source_target_pairs={{0,8},{1,9},{2,10},{3,11},{4,12},{5,13},{6,14},{7,15},{16,24},{17,... | collective-permute-start | bytes 1572872 | tf_op jit(solution)/shard_map/ppermute | solution.py:195
  34.0 5.1 %copy-start.1 = (s32[8,4]{0,1:T(4,128)S(1)}, s32[8,4]{0,1:T(4,128)}, u32[]{:S(2)}) copy-start(s32[8,4]{0,1:T(4,128)} %param.7) | copy-start | bytes 388
  34.0 8.1 %copy-start.2 = (f32[8,8]{1,0:T(8,128)S(1)}, f32[8,8]{1,0:T(8,128)}, u32[]{:S(2)}) copy-start(f32[8,8]{1,0:T(8,128)} %param.11) | copy-start | bytes 772
  39.3 4.9 %collective-permute-start.2 = (bf16[8,128,384]{2,1,0:T(8,128)(2,1)S(1)}, bf16[8,128,384]{2,1,0:T(8,128)(2,1)}, u32[]{:S(2)}, u32[]{:S(2)}) collective-permute-start(bf16[8,128,384]{2,1,0:T(8,128)(2,1)S(1)} %bitcast.26), channel_id=1, source_target_pairs={{0,1},{1,0},{2,3},{3,2},{4,5},{5,4},{6,7},{7,6},{8,9},{9,8},{10,11... | collective-permute-start | bytes 2359304 | tf_op jit(solution)/shard_map/ppermute | solution.py:199
  53.5 2.2 %copy-start = (bf16[128,16384]{1,0:T(8,128)(2,1)S(1)}, bf16[128,16384]{1,0:T(8,128)(2,1)}, u32[]{:S(2)}) copy-start(bf16[128,16384]{1,0:T(8,128)(2,1)} %flat.1.refs_4_.refs_3_) | copy-start | bytes 12582916
  61.0 14.9 %copy-start.3 = (bf16[128,512]{1,0:T(8,128)(2,1)S(1)}, bf16[128,512]{1,0:T(8,128)(2,1)}, u32[]{:S(2)}) copy-start(bf16[128,512]{1,0:T(8,128)(2,1)} %param.10) | copy-start | bytes 393220
  71.5 20.9 %all-to-all-start.1 = ((bf16[8,48,128]{2,1,0:T(8,128)(2,1)}), bf16[8,48,128]{2,1,0:T(8,128)(2,1)S(1)}, u32[]{:S(2)}, u32[]{:S(2)}) async-start(bf16[8,48,128]{2,1,0:T(8,128)(2,1)} %pad_maximum_fusion.1), calls=%async_computation.1 | async-start | bytes 196608 | tf_op jit(solution)/shard_map/all_to_all | solution.py:210
  75.9 16.5 %collective-permute-start.5 = (bf16[128,512]{1,0:T(8,128)(2,1)S(1)}, bf16[128,512]{1,0:T(8,128)(2,1)S(1)}, u32[]{:S(2)}, u32[]{:S(2)}) collective-permute-start(bf16[128,512]{1,0:T(8,128)(2,1)S(1)} %copy-done.3), channel_id=1, source_target_pairs={{8,16},{9,17},{10,18},{11,19},{12,20},{13,21},{14,22},{15,23},{24,... | collective-permute-start | bytes 393224 | tf_op jit(solution)/shard_map/ppermute | solution.py:196
  86.2 6.3 %collective-permute-start.4 = (bf16[128,512]{1,0:T(8,128)(2,1)S(1)}, bf16[128,512]{1,0:T(8,128)(2,1)S(1)}, u32[]{:S(2)}, u32[]{:S(2)}) collective-permute-start(bf16[128,512]{1,0:T(8,128)(2,1)S(1)} %copy-done.3), channel_id=1, source_target_pairs={{0,8},{1,9},{2,10},{3,11},{4,12},{5,13},{6,14},{7,15},{16,24},{17,... | collective-permute-start | bytes 393224 | tf_op jit(solution)/shard_map/ppermute | solution.py:197

commit v2 on v0

v2 whole, which is shorter than its diff:
```python
import functools

import jax
import jax.numpy as jnp
from jax import lax
from jax.experimental import pallas as pl
from jax.experimental.pallas import tpu as pltpu
from jax.sharding import PartitionSpec as P

SEGMENT = 8
NT = (((1,), (1,)), ((), ()))
VMEM = pl.BlockSpec(memory_space=pltpu.VMEM)
SMEM = pl.BlockSpec(memory_space=pltpu.SMEM)


def places():
    here, t = lax.axis_index("orb"), lax.axis_index("tm")
    place = lax.rem(here, SEGMENT)
    far = (place == 0) | (place == SEGMENT - 1)
    return lax.rem(here, 2), t, jnp.where(far, mirrored(lax.axis_size("tm"), t), t)


def mirrored(groups, t):
    return groups - 2 - t + 2 * (t % 2)


def prologue_kernel(block_map, integrals, occ, virt, coulomb, spread, own_out, far_out, rows, arrived, copied):
    share, orb, _ = far_out.shape
    place = places()[1:]
    copies = []
    for i in range(own_out.shape[0] - share):
        copies.append(
            pltpu.make_async_copy(coulomb.at[:, i * orb : (i + 1) * orb], own_out.at[share + i], arrived.at[2 + i])
        )
    for i in range(spread.shape[0]):
        for kind, tile in enumerate((occ, virt)):
            copies.append(pltpu.make_async_copy(tile, spread.at[i, kind], copied.at[i, kind]))
    loads = []
    for number in range(2):
        start = pl.multiple_of(place[number] * share, share)
        loads.append(
            pltpu.make_async_copy(integrals.at[pl.ds(start, share)], rows.at[number], arrived.at[number])
        )
    for copy in loads + copies:
        copy.start()
    blocks = block_map.shape[0]
    chunk = orb // blocks
    for number, out in ((1, far_out), (0, own_out)):
        loads[number].wait()
        for j in range(blocks):
            keep = block_map[j, place[number]].astype(jnp.float32)
            part = slice(j * chunk, (j + 1) * chunk)
            out[:share, part, :] = rows[number, :, part, :] * jnp.full((1, 1, orb), keep).astype(out.dtype)
    for copy in copies:
        copy.wait()


def prologue(block_map, integrals, occ, virt, coulomb, copies, share):
    orb = integrals.shape[1]
    lanes = coulomb.shape[1] // orb
    shape = lambda count: jax.ShapeDtypeStruct((count, orb, orb), integrals.dtype)
    return pl.pallas_call(
        prologue_kernel,
        out_shape=[jax.ShapeDtypeStruct((copies, 2) + occ.shape, occ.dtype), shape(share + lanes), shape(share)],
        in_specs=[pl.BlockSpec(memory_space=pltpu.SMEM)] + [pl.BlockSpec(memory_space=pltpu.HBM)] * 4,
        out_specs=[VMEM] * 3,
        scratch_shapes=[
            pltpu.VMEM((2, share, orb, orb), integrals.dtype),
            pltpu.SemaphoreType.DMA((2 + lanes,)),
            pltpu.SemaphoreType.DMA((copies, 2)),
        ],
    )(block_map.T, integrals, occ, virt, coulomb)


def cosine_weights(cosine, nq, nt, kind):
    core = lax.rem(lax.axis_index("tm"), 2)
    core = core if kind == 0 else 1 - core
    freqs = cosine.shape[0]
    row = lax.broadcasted_iota(jnp.int32, (freqs * nq, nt * nq), 0)
    col = lax.broadcasted_iota(jnp.int32, (freqs * nq, nt * nq), 1)
    block = jnp.where(row % nq == col % nq, (row // nq) * nt + col // nq, -1)
    full = jnp.zeros(row.shape, jnp.float32)
    for f in range(freqs):
        for y in range(nt):
            full = jnp.where(block == f * nt + y, cosine[f, 2 * y + core], full)
    terms = []
    for _ in range(3):
        term = full.astype(jnp.bfloat16)
        terms.append(term)
        full = full - term.astype(jnp.float32)
    return terms


def pair_and_respond(nq, jobs, selects, sources, tiles, own_far, block_map, cosine, half, pair, first):
    nt, _, orb, _ = tiles[0].shape
    step_rows = nq * nt
    rows = step_rows * len(jobs)
    pitch = orb + 8
    group = min(nq, 4)
    count = own_far.shape[0]
    if first:
        natural, wide, arrived, own_out = first
        fetch = pltpu.make_async_copy(own_far, natural, arrived)
        fetch.start()
    for number, (k, kind) in enumerate(jobs):
        if number == 1 and first:
            fetch.wait()
        source, tile = sources[k], tiles[kind]
        lane0 = pl.ds(pl.multiple_of(selects[k] * orb, orb), orb)
        for i in range(nt // 2):
            right = tile[2 * i : 2 * i + 2, 1, :, lane0].reshape(2 * orb, orb)
            for g in range(nq // group):
                left = source[g * group : (g + 1) * group].reshape(group * orb, orb)
                value = lax.dot_general(left, right, NT, preferred_element_type=jnp.float32)
                half[g * group : (g + 1) * group, :, 2 * i * orb : 2 * (i + 1) * orb] = (
                    value.astype(jnp.bfloat16).reshape(group, orb, 2 * orb)
                )
        for t in range(nt):
            if number > 0 and first:
                steps = nt * (len(jobs) - 1)
                step = nt * (number - 1) + t
                for p in range(count * step // steps, count * (step + 1) // steps):
                    wide[p * pitch : p * pitch + orb, :] = natural[p].astype(jnp.float32)
            left = tile[t, 0, :, lane0]
            for q in range(0, nq, 2):
                right = jnp.concatenate(
                    [half[q, :, t * orb : (t + 1) * orb], half[q + 1, :, t * orb : (t + 1) * orb]], axis=1
                )
                value = jnp.dot(left, right, preferred_element_type=jnp.float32)
                row = (number * step_rows + t * nq + q) * pitch
                pair[row : row + orb, :] = value[:, :orb]
                pair[row + pitch : row + pitch + orb, :] = value[:, orb:]
    blocks, row_blocks = block_map.shape
    chunk = orb // blocks
    column = lax.broadcasted_iota(jnp.int32, (1, count), 1) // (count // row_blocks)

    def response_step(c, total):
        left = jnp.concatenate(
            [pair[pl.ds(c * chunk + i, rows, stride=pitch), :].astype(jnp.bfloat16) for i in range(chunk)],
            axis=1,
        )
        lanes = pl.ds(pl.multiple_of(c * chunk * orb, chunk * orb), chunk * orb)
        if first:
            right = jnp.concatenate(
                [wide[pl.ds(c * chunk + i, count, stride=pitch), :].astype(jnp.bfloat16) for i in range(chunk)],
                axis=1,
            )
            own_out[:, lanes] = right
        else:
            right = own_far[:, lanes]
        value = lax.dot_general(left, right, NT, preferred_element_type=jnp.float32)
        keep = jnp.zeros((1, count), jnp.float32)
        for b in range(row_blocks):
            keep = jnp.where(column == b, block_map[c, b].astype(jnp.float32), keep)
        return total + value * keep

    total = lax.fori_loop(0, blocks, response_step, jnp.zeros((rows, count), jnp.float32))
    response = total.astype(jnp.bfloat16)
    weights = [cosine_weights(cosine, nq, nt, kind) for kind in range(len(tiles))]
    sums = [None] * len(sources)
    for number, (k, kind) in enumerate(jobs):
        piece = response[number * step_rows : (number + 1) * step_rows]
        for weight in weights[kind]:
            term = jnp.dot(weight, piece, preferred_element_type=jnp.float32)
            sums[k] = term if sums[k] is None else sums[k] + term
    return sums


def near_kernel(nq, own_share, beside, mine, other, integrals, block_map, cosine, out, own_out, half, pair, natural, wide, arrived):
    odd = lax.rem(lax.axis_index("orb"), 2)
    jobs = ((0, 0), (1, 0), (0, 1), (1, 1))
    sums = pair_and_respond(
        nq, jobs, (1, 2 - 2 * odd), (own_share, beside), (mine, other), integrals, block_map, cosine, half, pair,
        (natural, wide, arrived, own_out),
    )
    for k, value in enumerate(sums):
        out[k] = value


def below_kernel(nq, source, mine, other, own, block_map, cosine, out, half, pair):
    odd = lax.rem(lax.axis_index("orb"), 2)

    @pl.when(odd == 0)
    def _():
        jobs = ((0, 0), (0, 1))
        out[...] = pair_and_respond(
            nq, jobs, (0,), (source,), (mine, other), own, block_map, cosine, half, pair, None
        )[0]


def above_kernel(nq, source, mine, other, own, block_map, cosine, near, below, out, half, pair):
    odd = lax.rem(lax.axis_index("orb"), 2)

    def put(k, value):
        out[:, k * nq : (k + 1) * nq, :] = value.astype(out.dtype).reshape(-1, nq, value.shape[1])

    for k in range(near.shape[0]):
        put(k, near[k])

    @pl.when(odd == 0)
    def _():
        put(near.shape[0], below[...])

    @pl.when(odd == 1)
    def _():
        jobs = ((0, 0), (0, 1))
        value = pair_and_respond(
            nq, jobs, (2,), (source,), (mine, other), own, block_map, cosine, half, pair, None
        )
        put(near.shape[0], value[0])


def scratch(nq, tile, jobs):
    nt, _, orb, _ = tile.shape
    return [
        pltpu.VMEM((nq, orb, nt * orb), jnp.bfloat16),
        pltpu.VMEM((nq * nt * jobs * (orb + 8), orb), jnp.float32),
    ]


def near_call(nq, own_share, beside, mine, other, integrals, block_map, cosine):
    count, orb, _ = integrals.shape
    return pl.pallas_call(
        functools.partial(near_kernel, nq),
        out_shape=[
            jax.ShapeDtypeStruct((2, cosine.shape[0] * nq, count), jnp.float32),
            jax.ShapeDtypeStruct((count, orb * orb), integrals.dtype),
        ],
        in_specs=[VMEM] * 4 + [pl.BlockSpec(memory_space=pltpu.HBM)] + [SMEM] * 2,
        out_specs=[VMEM] * 2,
        scratch_shapes=scratch(nq, mine, 4)
        + [
            pltpu.VMEM(integrals.shape, integrals.dtype),
            pltpu.VMEM((count * (orb + 8), orb), jnp.float32),
            pltpu.SemaphoreType.DMA,
        ],
        compiler_params=pltpu.CompilerParams(vmem_limit_bytes=46 * 2**20),
    )(own_share, beside, mine, other, integrals, block_map.T, cosine)


def far_call(nq, source, mine, other, own, block_map, cosine, near=None, below=None):
    last = near is not None
    freqs, count = cosine.shape[0], own.shape[0]
    if last:
        out = jax.ShapeDtypeStruct((freqs, nq * (1 + near.shape[0]), count), jnp.bfloat16)
    else:
        out = jax.ShapeDtypeStruct((freqs * nq, count), jnp.float32)
    return pl.pallas_call(
        functools.partial(above_kernel if last else below_kernel, nq),
        out_shape=out,
        in_specs=[VMEM] * 4 + [SMEM] * 2 + [VMEM] * (2 if last else 0),
        out_specs=VMEM,
        scratch_shapes=scratch(nq, mine, 2),
        compiler_params=pltpu.CompilerParams(vmem_limit_bytes=20 * 2**20),
    )(source, mine, other, own, block_map.T, cosine, *((near, below) if last else ()))


AXES = ("orb", "tm")


def chain_pairs(domains, groups, first, step):
    pairs = []
    for here in range(first, domains, 2):
        there = (here + step) % domains
        far = here // SEGMENT != there // SEGMENT
        for t in range(groups):
            pairs.append((here * groups + t, there * groups + (mirrored(groups, t) if far else t)))
    return pairs


def body(integrals, block_map, green_occ, green_virt, coulomb, cosine):
    return steps(integrals, block_map, green_occ[0], green_virt[0], coulomb, cosine)


def steps(integrals, block_map, occ_own, virt_own, coulomb, cosine):
    aux_rows, _, _ = integrals.shape
    groups = lax.axis_size("tm")
    domains = lax.axis_size("orb")
    share = aux_rows // groups
    up = chain_pairs(domains, groups, 1, 1)
    down = chain_pairs(domains, groups, 0, -1)
    even = chain_pairs(domains, groups, 0, 1) + chain_pairs(domains, groups, 1, -1)
    twin = [(i, i ^ 1) for i in range(groups)]
    lines = [list(range(c, groups, 2)) for c in range(2)]
    spread, own_share, far_share = prologue(
        block_map, integrals, occ_own, virt_own, coulomb, groups // 2, share
    )
    from_below = lax.ppermute(far_share, AXES, up)
    mine = lax.all_to_all(spread, "tm", split_axis=0, concat_axis=0, tiled=True, axis_index_groups=lines)
    source_a = lax.ppermute(own_share, AXES, even)
    from_above = lax.ppermute(far_share, AXES, down)
    coulomb_b = lax.ppermute(coulomb, AXES, up + down)
    coulomb_a = source_a[share:].transpose(1, 0, 2).reshape(aux_rows, -1)
    other = lax.ppermute(mine, "tm", twin)
    near, own = near_call(share, own_share, source_a, mine, other, integrals, block_map, cosine)
    below = far_call(share, from_below, mine, other, own, block_map, cosine)
    mixed = far_call(share, from_above, mine, other, own, block_map, cosine, near, below)
    mixed = lax.all_to_all(mixed, "tm", split_axis=0, concat_axis=0, tiled=True)
    columns = jnp.concatenate(
        [c.reshape(groups, share, c.shape[1]) for c in (coulomb, coulomb_a, coulomb_b)], axis=1
    )
    columns = lax.optimization_barrier(columns)
    return lax.dot_general(
        mixed.reshape(-1, aux_rows),
        columns.reshape(-1, coulomb.shape[1]),
        (((0,), (0,)), ((), ())),
        preferred_element_type=jnp.float32,
    )[None]


def solution(mesh):
    in_specs = (
        P("orb", None, None),
        P("orb", None),
        P("tm", "orb", None),
        P("tm", "orb", None),
        P("orb", None),
        P(),
    )
    out_specs = P("tm", "orb", None)
    return jax.shard_map(body, mesh=mesh, in_specs=in_specs, out_specs=out_specs, check_vma=False)
```

time: 260 us -> 93.2 us (0.36)
  waiting for transfers between devices: 100 us -> 15.2 us
  local copies, waits for them, and re-layouts: 50 us -> 1.26 us
  matrix products: 36.2 us -> 0.96 us
  Pallas kernels: 0 us -> 22 us
  other arithmetic: 15.1 us -> 0.03 us
  between operations: 13.6 us -> 0.16 us
  starting transfers between devices: 21.2 us -> 29.4 us
    all_gather x1 -> x0, waiting for transfers between devices: 77.8 us -> none  [body(): whole_rims = lax.all_gather(rim_pair, 'tm', axis=1, tiled=True)]
    dot_general x7 -> x1, matrix products: 36.2 us -> 0.96 us  [steps(): lax.dot_general(mixed.reshape(-1, aux_rows), columns.reshape(-1, coulomb....]
    pallas_call x0 -> x4, Pallas kernels: none -> 22 us  [the longest x1 11.2 us: near_call(): pl.pallas_call(functools.partial(near_kernel, nq), out_shape=[jax.ShapeDt...]
    convert_element_type x4 -> x0, local copies, waits for them, and re-layouts: 20.4 us -> none  [the longest x3 20.3 us: body(): pair_side = jnp.einsum('ml,qln->qmn', occ_tiles[:, offset, :], half_side,...]
    unnamed x21 -> x8, local copies, waits for them, and re-layouts: 14.2 us -> 1.09 us
    ppermute x2 -> x5, waiting for transfers between devices: 22.3 us -> 10.1 us  [the longest x1 10.1 us: steps(): from_below = lax.ppermute(far_share, AXES, up)]
    mul x2 -> x0, other arithmetic: 11.8 us -> none  [body(): masked = (shaped * keep_mask).reshape(aux_rows, pair_count)]
    mul x4 -> x0, local copies, waits for them, and re-layouts: 10.4 us -> none  [body(): masked = (shaped * keep_mask).reshape(aux_rows, pair_count)]
  transfers between devices with their start and end apart: 3 -> 6, of which waited for: 3 -> 2; matrix products, arithmetic and copies ran while one was open for 7% -> 0% of each run, Pallas kernels for 0% -> 20%
where the time goes in v2:
time: 93.2 us; the launch traced here: 92.8 us
  starting transfers between devices  29.4 us (32%)
  blocking collectives  23.8 us (26%)
  Pallas kernels  22 us (24%)
  waiting for transfers between devices  15.2 us (16%)
  local copies, waits for them, and re-layouts  1.26 us (1%)
  matrix products  0.96 us (1%)
    all_to_all x1, blocking collectives, steps(): lax.all_to_all(spread, 'tm', split_axis=0, concat_axis=0, tiled=True, axi...  23.8 us
    ppermute x1, starting transfers between devices, steps(): from_above = lax.ppermute(far_share, AXES, down)  13.4 us
    pallas_call x1, Pallas kernels, near_call(): pl.pallas_call(functools.partial(near_kernel, nq), out_shape=[jax.ShapeDt...  11.2 us
    ppermute x1, waiting for transfers between devices, steps(): from_below = lax.ppermute(far_share, AXES, up)  10.1 us
    pallas_call x2, Pallas kernels, far_call(): pl.pallas_call(functools.partial(above_kernel if last else below_kernel,...  7.05 us
    all_to_all x1, waiting for transfers between devices, steps(): mixed = lax.all_to_all(mixed, 'tm', split_axis=0, concat_axis=0, tiled=True)  5.13 us
    ppermute x1, starting transfers between devices, steps(): other = lax.ppermute(mine, 'tm', twin)  4.6 us
    all_to_all x1, starting transfers between devices, steps(): mixed = lax.all_to_all(mixed, 'tm', split_axis=0, concat_axis=0, tiled=True)  4.12 us
  transfers between devices with their start and end apart: 6, of which 2 were waited for; matrix products, arithmetic and copies ran while one was open for 0% of the time, Pallas kernels for 20%

profile of v2, /device:TPU:1, one launch (start us, length us, event | category | flops | bytes accessed | tf_op | source)
XLA Modules:
  0.0 92.8 jit_solution(1561422333120695323)
XLA Ops:
  0.0 0.0 copy-start.2
  0.0 0.0 copy-start.3
  0.0 0.0 copy-start.1
  0.0 3.7 %shard_map.64 = (bf16[4,2,128,384]{3,2,1,0:T(8,128)(2,1)}, bf16[20,128,128]{2,1,0:T(8,128)(2,1)}, bf16[16,128,128]{2,1,0:T(8,128)(2,1)}) custom-call(s32[4,8]{1,0:T(4,128)} %bitcast.12, bf16[128,128,128]{2,1,0:T(8,128)(2,1)} %integrals.3, bf16[128,384]{1,0:T(8,128)(2,1)} %bitcast.18, bf16[128,384]{1,0:T(8,128)(2,1)} %bitcast.19, bf16[128,512]{1,0:T(8,128)(2,1)} %coulomb.1), custom_call_target="tpu_custom_call" | custom-call | tf_op jit(solution)/shard_map/pallas_call | solution.py:62
  3.7 23.8 %all_to_all.10.mine = bf16[4,2,128,384]{3,2,1,0:T(8,128)(2,1)S(1)} all-to-all(bf16[4,2,128,384]{3,2,1,0:T(8,128)(2,1)} %get-tuple-element.11), channel_id=1, replica_groups={{0,2,4,6},{1,3,5,7},{8,10,12,14},{9,11,13,15},{16,18,20,22},{17,19,21,2..., dimensions={0} | all-to-all | bytes 1572864 | tf_op jit(solution)/shard_map/all_to_all | solution.py:289
  27.5 4.6 %collective-permute-start.1 = (bf16[4,2,128,384]{3,2,1,0:T(8,128)(2,1)S(1)}, bf16[4,2,128,384]{3,2,1,0:T(8,128)(2,1)S(1)}, u32[]{:S(2)}, u32[]{:S(2)}) collective-permute-start(bf16[4,2,128,384]{3,2,1,0:T(8,128)(2,1)S(1)} %all_to_all.10.mine), channel_id=1, source_target_pairs={{0,1},{1,0},{2,3},{3,2},{4,5},{5,4},{6,7},{7,6},{8,9},{9,8},{10,11... | collective-permute-start | bytes 2359304 | tf_op jit(solution)/shard_map/ppermute | solution.py:294
  32.1 4.0 %collective-permute-start.2 = (bf16[20,128,128]{2,1,0:T(8,128)(2,1)}, bf16[20,128,128]{2,1,0:T(8,128)(2,1)S(1)}, u32[]{:S(2)}, u32[]{:S(2)}) collective-permute-start(bf16[20,128,128]{2,1,0:T(8,128)(2,1)} %get-tuple-element.12.own_share), channel_id=1, source_target_pairs={{0,8},{1,9},{2,10},{3,11},{4,12},{5,13},{6,14},{7,15},{16,24},{17,... | collective-permute-start | bytes 1966088 | tf_op jit(solution)/shard_map/ppermute | solution.py:290
  36.2 1.3 %collective-permute-start.3 = (bf16[16,128,128]{2,1,0:T(8,128)(2,1)}, bf16[16,128,128]{2,1,0:T(8,128)(2,1)S(1)}, u32[]{:S(2)}, u32[]{:S(2)}) collective-permute-start(bf16[16,128,128]{2,1,0:T(8,128)(2,1)} %get-tuple-element.10), channel_id=1, source_target_pairs={{8,16},{9,17},{10,18},{11,19},{12,20},{13,21},{14,22},{15,23},{24,... | collective-permute-start | bytes 1572872 | tf_op jit(solution)/shard_map/ppermute | solution.py:288
  37.5 13.4 %collective-permute-start = (bf16[16,128,128]{2,1,0:T(8,128)(2,1)}, bf16[16,128,128]{2,1,0:T(8,128)(2,1)S(1)}, u32[]{:S(2)}, u32[]{:S(2)}) collective-permute-start(bf16[16,128,128]{2,1,0:T(8,128)(2,1)} %get-tuple-element.10), channel_id=1, source_target_pairs={{0,510},{1,511},{2,508},{3,509},{4,506},{5,507},{6,504},{7,505},{1... | collective-permute-start | bytes 1572872 | tf_op jit(solution)/shard_map/ppermute | solution.py:291
  50.9 0.0 copy-done.3
  50.9 1.9 %collective-permute-start.4 = (bf16[128,512]{1,0:T(8,128)(2,1)S(1)}, bf16[128,512]{1,0:T(8,128)(2,1)S(1)}, u32[]{:S(2)}, u32[]{:S(2)}) collective-permute-start(bf16[128,512]{1,0:T(8,128)(2,1)S(1)} %copy-done.3), channel_id=1, source_target_pairs={{8,16},{9,17},{10,18},{11,19},{12,20},{13,21},{14,22},{15,23},{24,... | collective-permute-start | bytes 393224 | tf_op jit(solution)/shard_map/ppermute | solution.py:292
  52.9 0.0 collective-permute-done.2.beside
  52.9 0.0 collective-permute-done.1.other
  52.9 0.0 copy-done.2
  52.9 0.0 copy-done.1
  52.9 0.0 copy-start
  52.9 1.1 %copy-done = bf16[20,128,128]{2,1,0:T(8,128)(2,1)S(1)} copy-done((bf16[20,128,128]{2,1,0:T(8,128)(2,1)S(1)}, bf16[20,128,128]{2,1,0:T(8,128)(2,1)}, u32[]{:S(2)}) %copy-start) | copy-done | bytes 655384
  54.0 11.2 %shard_map.65 = (f32[2,128,128]{2,1,0:T(8,128)S(1)}, bf16[128,16384]{1,0:T(8,128)(2,1)S(1)}) custom-call(bf16[20,128,128]{2,1,0:T(8,128)(2,1)S(1)} %copy-done, bf16[20,128,128]{2,1,0:T(8,128)(2,1)S(1)} %collective-permute-done.2.beside, bf16[4,2,128,384]{3,2,1,0:T(8,128)(2,1)S(1)} %all_to_all.10.mine, ...), custom_call_target="tpu_custom_call" | custom-call | tf_op jit(solution)/shard_map/pallas_call | solution.py:223
  65.2 10.1 %collective-permute-done.3.source = bf16[16,128,128]{2,1,0:T(8,128)(2,1)S(1)} collective-permute-done((bf16[16,128,128]{2,1,0:T(8,128)(2,1)}, bf16[16,128,128]{2,1,0:T(8,128)(2,1)S(1)}, u32[]{:S(2)}, u32[]{:S(2)}) %collective-permute-start.3) | collective-permute-done | bytes 524320 | tf_op jit(solution)/shard_map/ppermute | solution.py:288
  75.3 5.6 %shard_map.66.below = f32[128,128]{1,0:T(8,128)S(1)} custom-call(bf16[16,128,128]{2,1,0:T(8,128)(2,1)S(1)} %collective-permute-done.3.source, bf16[4,2,128,384]{3,2,1,0:T(8,128)(2,1)S(1)} %all_to_all.10.mine, bf16[4,2,128,384]{3,2,1,0:T(8,128)(2,1)S(1)} %collective-permute-done.1.other, bf16[128,16384]{1,0:T(8,128)(2,1)S(1)} %get-tuple-element.13.own, ...), custom_call_target="tpu_custom_call" | custom-call | tf_op jit(solution)/shard_map/pallas_call | solution.py:248
  80.8 0.0 collective-permute-done.source
  80.9 1.5 %shard_map.67 = bf16[8,48,128]{2,1,0:T(8,128)(2,1)} custom-call(bf16[16,128,128]{2,1,0:T(8,128)(2,1)S(1)} %collective-permute-done.source, bf16[4,2,128,384]{3,2,1,0:T(8,128)(2,1)S(1)} %all_to_all.10.mine, bf16[4,2,128,384]{3,2,1,0:T(8,128)(2,1)S(1)} %collective-permute-done.1.other, bf16[128,16384]{1,0:T(8,128)(2,1)S(1)} %get-tuple-element.13.own, ...), custom_call_target="tpu_custom_call" | custom-call | tf_op jit(solution)/shard_map/pallas_call | solution.py:248
  82.3 4.1 %all-to-all-start.1 = ((bf16[8,48,128]{2,1,0:T(8,128)(2,1)}), bf16[8,48,128]{2,1,0:T(8,128)(2,1)S(1)}, u32[]{:S(2)}, u32[]{:S(2)}) async-start(bf16[8,48,128]{2,1,0:T(8,128)(2,1)} %shard_map.67), calls=%async_computation.1 | async-start | bytes 196608 | tf_op jit(solution)/shard_map/all_to_all | solution.py:298
  86.5 0.1 copy.7
  86.6 0.1 reshape_reshape.3
  86.6 0.0 collective-permute-done.4
  86.7 5.1 %all-to-all-done.1 = bf16[8,48,128]{2,1,0:T(8,128)(2,1)S(1)} async-done(((bf16[8,48,128]{2,1,0:T(8,128)(2,1)}), bf16[8,48,128]{2,1,0:T(8,128)(2,1)S(1)}, u32[]{:S(2)}, u32[]{:S(2)}) %all-to-all-start.1) | async-done | bytes 98336 | tf_op jit(solution)/shard_map/all_to_all | solution.py:298
  91.8 1.0 %convolution_bitcast_fusion = f32[1,128,512]{2,1,0:T(8,128)} fusion(bf16[8,48,128]{2,1,0:T(8,128)(2,1)S(1)} %all-to-all-done.1, bf16[8,48,512]{2,1,0:T(8,128)(2,1)S(1)} %pad_maximum_fusion), kind=kOutput, calls=%fused_computation | convolution fusion | flops 50331648 | bytes 753664 | tf_op jit(solution)/shard_map/dot_general | solution.py:303
  (2 shorter events, 0.0 us)
Async XLA Ops:
  0.0 52.9 %copy-start.2 = (s32[8,4]{0,1:T(4,128)S(1)}, s32[8,4]{0,1:T(4,128)}, u32[]{:S(2)}) copy-start(s32[8,4]{0,1:T(4,128)} %param.7) | copy-start | bytes 388
  0.0 50.9 %copy-start.3 = (bf16[128,512]{1,0:T(8,128)(2,1)S(1)}, bf16[128,512]{1,0:T(8,128)(2,1)}, u32[]{:S(2)}) copy-start(bf16[128,512]{1,0:T(8,128)(2,1)} %coulomb.1) | copy-start | bytes 393220
  0.0 52.9 %copy-start.1 = (f32[8,8]{1,0:T(8,128)S(1)}, f32[8,8]{1,0:T(8,128)}, u32[]{:S(2)}) copy-start(f32[8,8]{1,0:T(8,128)} %cosine.5) | copy-start | bytes 772
  27.5 25.3 %collective-permute-start.1 = (bf16[4,2,128,384]{3,2,1,0:T(8,128)(2,1)S(1)}, bf16[4,2,128,384]{3,2,1,0:T(8,128)(2,1)S(1)}, u32[]{:S(2)}, u32[]{:S(2)}) collective-permute-start(bf16[4,2,128,384]{3,2,1,0:T(8,128)(2,1)S(1)} %all_to_all.10.mine), channel_id=1, source_target_pairs={{0,1},{1,0},{2,3},{3,2},{4,5},{5,4},{6,7},{7,6},{8,9},{9,8},{10,11... | collective-permute-start | bytes 2359304 | tf_op jit(solution)/shard_map/ppermute | solution.py:294
  32.1 20.7 %collective-permute-start.2 = (bf16[20,128,128]{2,1,0:T(8,128)(2,1)}, bf16[20,128,128]{2,1,0:T(8,128)(2,1)S(1)}, u32[]{:S(2)}, u32[]{:S(2)}) collective-permute-start(bf16[20,128,128]{2,1,0:T(8,128)(2,1)} %get-tuple-element.12.own_share), channel_id=1, source_target_pairs={{0,8},{1,9},{2,10},{3,11},{4,12},{5,13},{6,14},{7,15},{16,24},{17,... | collective-permute-start | bytes 1966088 | tf_op jit(solution)/shard_map/ppermute | solution.py:290
  36.2 39.1 %collective-permute-start.3 = (bf16[16,128,128]{2,1,0:T(8,128)(2,1)}, bf16[16,128,128]{2,1,0:T(8,128)(2,1)S(1)}, u32[]{:S(2)}, u32[]{:S(2)}) collective-permute-start(bf16[16,128,128]{2,1,0:T(8,128)(2,1)} %get-tuple-element.10), channel_id=1, source_target_pairs={{8,16},{9,17},{10,18},{11,19},{12,20},{13,21},{14,22},{15,23},{24,... | collective-permute-start | bytes 1572872 | tf_op jit(solution)/shard_map/ppermute | solution.py:288
  37.5 43.4 %collective-permute-start = (bf16[16,128,128]{2,1,0:T(8,128)(2,1)}, bf16[16,128,128]{2,1,0:T(8,128)(2,1)S(1)}, u32[]{:S(2)}, u32[]{:S(2)}) collective-permute-start(bf16[16,128,128]{2,1,0:T(8,128)(2,1)} %get-tuple-element.10), channel_id=1, source_target_pairs={{0,510},{1,511},{2,508},{3,509},{4,506},{5,507},{6,504},{7,505},{1... | collective-permute-start | bytes 1572872 | tf_op jit(solution)/shard_map/ppermute | solution.py:291
  50.9 35.7 %collective-permute-start.4 = (bf16[128,512]{1,0:T(8,128)(2,1)S(1)}, bf16[128,512]{1,0:T(8,128)(2,1)S(1)}, u32[]{:S(2)}, u32[]{:S(2)}) collective-permute-start(bf16[128,512]{1,0:T(8,128)(2,1)S(1)} %copy-done.3), channel_id=1, source_target_pairs={{8,16},{9,17},{10,18},{11,19},{12,20},{13,21},{14,22},{15,23},{24,... | collective-permute-start | bytes 393224 | tf_op jit(solution)/shard_map/ppermute | solution.py:292
  52.9 1.1 %copy-start = (bf16[20,128,128]{2,1,0:T(8,128)(2,1)S(1)}, bf16[20,128,128]{2,1,0:T(8,128)(2,1)}, u32[]{:S(2)}) copy-start(bf16[20,128,128]{2,1,0:T(8,128)(2,1)} %get-tuple-element.12.own_share) | copy-start | bytes 1966084
  82.3 9.5 %all-to-all-start.1 = ((bf16[8,48,128]{2,1,0:T(8,128)(2,1)}), bf16[8,48,128]{2,1,0:T(8,128)(2,1)S(1)}, u32[]{:S(2)}, u32[]{:S(2)}) async-start(bf16[8,48,128]{2,1,0:T(8,128)(2,1)} %shard_map.67), calls=%async_computation.1 | async-start | bytes 196608 | tf_op jit(solution)/shard_map/all_to_all | solution.py:298

commit v3 on v2

--- a/solution.py
+++ b/solution.py
@@ -24,34 +24,49 @@
     return groups - 2 - t + 2 * (t % 2)
 
 
-def prologue_kernel(block_map, integrals, occ, virt, coulomb, spread, own_out, far_out, rows, arrived, copied):
+def prologue_kernel(block_map, integrals, occ, virt, coulomb, spread, own_out, far_out, tiles, rows, arrived, copied):
     share, orb, _ = far_out.shape
     place = places()[1:]
-    copies = []
-    for i in range(own_out.shape[0] - share):
-        copies.append(
-            pltpu.make_async_copy(coulomb.at[:, i * orb : (i + 1) * orb], own_out.at[share + i], arrived.at[2 + i])
-        )
-    for i in range(spread.shape[0]):
-        for kind, tile in enumerate((occ, virt)):
-            copies.append(pltpu.make_async_copy(tile, spread.at[i, kind], copied.at[i, kind]))
-    loads = []
+    lanes = own_out.shape[0] - share
+    loads = [
+        pltpu.make_async_copy(occ, tiles.at[0], arrived.at[0]),
+        pltpu.make_async_copy(virt, tiles.at[1], arrived.at[1]),
+    ]
     for number in range(2):
         start = pl.multiple_of(place[number] * share, share)
         loads.append(
-            pltpu.make_async_copy(integrals.at[pl.ds(start, share)], rows.at[number], arrived.at[number])
+            pltpu.make_async_copy(
+                integrals.at[pl.ds(start, share)], rows.at[number, pl.ds(0, share)], arrived.at[2 + number]
+            )
         )
-    for copy in loads + copies:
+    for i in range(lanes):
+        loads.append(
+            pltpu.make_async_copy(
+                coulomb.at[:, i * orb : (i + 1) * orb], rows.at[0, share + i], arrived.at[4 + i]
+            )
+        )
+    stores = [pltpu.make_async_copy(tiles, spread.at[i], copied.at[i]) for i in range(spread.shape[0])]
+    stores.append(pltpu.make_async_copy(rows.at[1, pl.ds(0, share)], far_out, copied.at[len(stores)]))
+    stores.append(pltpu.make_async_copy(rows.at[0], own_out, copied.at[len(stores)]))
+    for copy in loads:
+        copy.start()
+    for copy in loads[:2]:
+        copy.wait()
+    for copy in stores[:-2]:
         copy.start()
     blocks = block_map.shape[0]
     chunk = orb // blocks
-    for number, out in ((1, far_out), (0, own_out)):
-        loads[number].wait()
+    for number in (1, 0):
+        loads[2 + number].wait()
         for j in range(blocks):
             keep = block_map[j, place[number]].astype(jnp.float32)
             part = slice(j * chunk, (j + 1) * chunk)
-            out[:share, part, :] = rows[number, :, part, :] * jnp.full((1, 1, orb), keep).astype(out.dtype)
-    for copy in copies:
+            rows[number, :share, part, :] = rows[number, :share, part, :] * jnp.full((1, 1, orb), keep).astype(rows.dtype)
+        if number == 0:
+            for copy in loads[4:]:
+                copy.wait()
+        stores[-1 - number].start()
+    for copy in stores:
         copy.wait()
 
 
@@ -59,15 +74,17 @@
     orb = integrals.shape[1]
     lanes = coulomb.shape[1] // orb
     shape = lambda count: jax.ShapeDtypeStruct((count, orb, orb), integrals.dtype)
+    far = pl.BlockSpec(memory_space=pltpu.HBM)
     return pl.pallas_call(
         prologue_kernel,
         out_shape=[jax.ShapeDtypeStruct((copies, 2) + occ.shape, occ.dtype), shape(share + lanes), shape(share)],
-        in_specs=[pl.BlockSpec(memory_space=pltpu.SMEM)] + [pl.BlockSpec(memory_space=pltpu.HBM)] * 4,
-        out_specs=[VMEM] * 3,
+        in_specs=[SMEM] + [far] * 4,
+        out_specs=[far] * 3,
         scratch_shapes=[
-            pltpu.VMEM((2, share, orb, orb), integrals.dtype),
-            pltpu.SemaphoreType.DMA((2 + lanes,)),
-            pltpu.SemaphoreType.DMA((copies, 2)),
+            pltpu.VMEM((2,) + occ.shape, occ.dtype),
+            pltpu.VMEM((2, share + lanes, orb, orb), integrals.dtype),
+            pltpu.SemaphoreType.DMA((4 + lanes,)),
+            pltpu.SemaphoreType.DMA((copies + 2,)),
         ],
     )(block_map.T, integrals, occ, virt, coulomb)
 
@@ -91,12 +108,15 @@
     return terms
 
 
-def pair_and_respond(nq, jobs, selects, sources, tiles, own_far, block_map, cosine, half, pair, first):
+def pair_and_respond(nq, jobs, selects, sources, tiles, own_far, block_map, cosine, half, pair, mixing, first):
+    for kind in range(len(tiles)):
+        for i, term in enumerate(cosine_weights(cosine, nq, tiles[0].shape[0], kind)):
+            mixing[kind, i] = term
     nt, _, orb, _ = tiles[0].shape
     step_rows = nq * nt
     rows = step_rows * len(jobs)
     pitch = orb + 8
-    group = min(nq, 4)
+    group = min(nq, 8)
     count = own_far.shape[0]
     if first:
         natural, wide, arrived, own_out = first
@@ -106,11 +126,22 @@
         if number == 1 and first:
             fetch.wait()
         source, tile = sources[k], tiles[kind]
+        if source is None:
+            me = lax.axis_index("tm")
+            line = lax.broadcasted_iota(jnp.int32, (1, orb, orb), 1) // (orb // block_map.shape[0])
+            mask = jnp.zeros((1, orb, orb), jnp.float32)
+            for j in range(block_map.shape[0]):
+                mask = jnp.where(line == j, block_map[j, me].astype(jnp.float32), mask)
+            mask = mask.astype(jnp.bfloat16)
         lane0 = pl.ds(pl.multiple_of(selects[k] * orb, orb), orb)
         for i in range(nt // 2):
             right = tile[2 * i : 2 * i + 2, 1, :, lane0].reshape(2 * orb, orb)
             for g in range(nq // group):
-                left = source[g * group : (g + 1) * group].reshape(group * orb, orb)
+                if source is None:
+                    left = natural[pl.ds(me * nq + g * group, group)] * mask
+                else:
+                    left = source[g * group : (g + 1) * group]
+                left = left.reshape(group * orb, orb)
                 value = lax.dot_general(left, right, NT, preferred_element_type=jnp.float32)
                 half[g * group : (g + 1) * group, :, 2 * i * orb : 2 * (i + 1) * orb] = (
                     value.astype(jnp.bfloat16).reshape(group, orb, 2 * orb)
@@ -154,41 +185,40 @@
             keep = jnp.where(column == b, block_map[c, b].astype(jnp.float32), keep)
         return total + value * keep
 
-    total = lax.fori_loop(0, blocks, response_step, jnp.zeros((rows, count), jnp.float32))
+    total = lax.fori_loop(0, blocks, response_step, jnp.zeros((rows, count), jnp.float32), unroll=4)
     response = total.astype(jnp.bfloat16)
-    weights = [cosine_weights(cosine, nq, nt, kind) for kind in range(len(tiles))]
     sums = [None] * len(sources)
     for number, (k, kind) in enumerate(jobs):
         piece = response[number * step_rows : (number + 1) * step_rows]
-        for weight in weights[kind]:
-            term = jnp.dot(weight, piece, preferred_element_type=jnp.float32)
+        for i in range(mixing.shape[1]):
+            term = jnp.dot(mixing[kind, i], piece, preferred_element_type=jnp.float32)
             sums[k] = term if sums[k] is None else sums[k] + term
     return sums
 
 
-def near_kernel(nq, own_share, beside, mine, other, integrals, block_map, cosine, out, own_out, half, pair, natural, wide, arrived):
+def near_kernel(nq, beside, mine, other, integrals, block_map, cosine, out, own_out, half, pair, mixing, natural, wide, arrived):
     odd = lax.rem(lax.axis_index("orb"), 2)
-    jobs = ((0, 0), (1, 0), (0, 1), (1, 1))
+    jobs = ((1, 0), (0, 0), (1, 1), (0, 1))
     sums = pair_and_respond(
-        nq, jobs, (1, 2 - 2 * odd), (own_share, beside), (mine, other), integrals, block_map, cosine, half, pair,
+        nq, jobs, (1, 2 - 2 * odd), (None, beside), (mine, other), integrals, block_map, cosine, half, pair, mixing,
         (natural, wide, arrived, own_out),
     )
     for k, value in enumerate(sums):
         out[k] = value
 
 
-def below_kernel(nq, source, mine, other, own, block_map, cosine, out, half, pair):
+def below_kernel(nq, source, mine, other, own, block_map, cosine, out, half, pair, mixing):
     odd = lax.rem(lax.axis_index("orb"), 2)
 
     @pl.when(odd == 0)
     def _():
         jobs = ((0, 0), (0, 1))
         out[...] = pair_and_respond(
-            nq, jobs, (0,), (source,), (mine, other), own, block_map, cosine, half, pair, None
+            nq, jobs, (0,), (source,), (mine, other), own, block_map, cosine, half, pair, mixing, None
         )[0]
 
 
-def above_kernel(nq, source, mine, other, own, block_map, cosine, near, below, out, half, pair):
+def above_kernel(nq, source, mine, other, own, block_map, cosine, near, below, out, half, pair, mixing):
     odd = lax.rem(lax.axis_index("orb"), 2)
 
     def put(k, value):
@@ -205,20 +235,21 @@
     def _():
         jobs = ((0, 0), (0, 1))
         value = pair_and_respond(
-            nq, jobs, (2,), (source,), (mine, other), own, block_map, cosine, half, pair, None
+            nq, jobs, (2,), (source,), (mine, other), own, block_map, cosine, half, pair, mixing, None
         )
         put(near.shape[0], value[0])
 
 
-def scratch(nq, tile, jobs):
+def scratch(nq, tile, jobs, freqs):
     nt, _, orb, _ = tile.shape
     return [
         pltpu.VMEM((nq, orb, nt * orb), jnp.bfloat16),
         pltpu.VMEM((nq * nt * jobs * (orb + 8), orb), jnp.float32),
+        pltpu.VMEM((2, 3, freqs * nq, nt * nq), jnp.bfloat16),
     ]
 
 
-def near_call(nq, own_share, beside, mine, other, integrals, block_map, cosine):
+def near_call(nq, beside, mine, other, integrals, block_map, cosine):
     count, orb, _ = integrals.shape
     return pl.pallas_call(
         functools.partial(near_kernel, nq),
@@ -226,16 +257,16 @@
             jax.ShapeDtypeStruct((2, cosine.shape[0] * nq, count), jnp.float32),
             jax.ShapeDtypeStruct((count, orb * orb), integrals.dtype),
         ],
-        in_specs=[VMEM] * 4 + [pl.BlockSpec(memory_space=pltpu.HBM)] + [SMEM] * 2,
+        in_specs=[VMEM] * 3 + [pl.BlockSpec(memory_space=pltpu.HBM)] + [SMEM] * 2,
         out_specs=[VMEM] * 2,
-        scratch_shapes=scratch(nq, mine, 4)
+        scratch_shapes=scratch(nq, mine, 4, cosine.shape[0])
         + [
             pltpu.VMEM(integrals.shape, integrals.dtype),
             pltpu.VMEM((count * (orb + 8), orb), jnp.float32),
             pltpu.SemaphoreType.DMA,
         ],
         compiler_params=pltpu.CompilerParams(vmem_limit_bytes=46 * 2**20),
-    )(own_share, beside, mine, other, integrals, block_map.T, cosine)
+    )(beside, mine, other, integrals, block_map.T, cosine)
 
 
 def far_call(nq, source, mine, other, own, block_map, cosine, near=None, below=None):
@@ -250,7 +281,7 @@
         out_shape=out,
         in_specs=[VMEM] * 4 + [SMEM] * 2 + [VMEM] * (2 if last else 0),
         out_specs=VMEM,
-        scratch_shapes=scratch(nq, mine, 2),
+        scratch_shapes=scratch(nq, mine, 2, freqs),
         compiler_params=pltpu.CompilerParams(vmem_limit_bytes=20 * 2**20),
     )(source, mine, other, own, block_map.T, cosine, *((near, below) if last else ()))
 
@@ -292,7 +323,7 @@
     coulomb_b = lax.ppermute(coulomb, AXES, up + down)
     coulomb_a = source_a[share:].transpose(1, 0, 2).reshape(aux_rows, -1)
     other = lax.ppermute(mine, "tm", twin)
-    near, own = near_call(share, own_share, source_a, mine, other, integrals, block_map, cosine)
+    near, own = near_call(share, source_a, mine, other, integrals, block_map, cosine)
     below = far_call(share, from_below, mine, other, own, block_map, cosine)
     mixed = far_call(share, from_above, mine, other, own, block_map, cosine, near, below)
     mixed = lax.all_to_all(mixed, "tm", split_axis=0, concat_axis=0, tiled=True)

time: 93.2 us -> 92.5 us (level)
  local copies, waits for them, and re-layouts: 1.26 us -> 0.18 us
    unnamed x8 -> x6, local copies, waits for them, and re-layouts: 1.09 us -> 0.01 us
    pallas_call x1, Pallas kernels: 11.2 us -> 12.2 us  [near_call(): pl.pallas_call(functools.partial(near_kernel, nq), out_shape=[jax.ShapeDt...]
where the time goes in v3:
time: 92.5 us; the launch traced here: 92 us
  starting transfers between devices  29.6 us (32%)
  blocking collectives  23.8 us (26%)
  Pallas kernels  22.1 us (24%)
  waiting for transfers between devices  15.3 us (17%)
  matrix products  0.95 us (1%)
    all_to_all x1, blocking collectives, steps(): lax.all_to_all(spread, 'tm', split_axis=0, concat_axis=0, tiled=True, axi...  23.8 us
    ppermute x1, starting transfers between devices, steps(): from_above = lax.ppermute(far_share, AXES, down)  13.4 us
    pallas_call x1, Pallas kernels, near_call(): pl.pallas_call(functools.partial(near_kernel, nq), out_shape=[jax.ShapeDt...  12.2 us
    ppermute x1, waiting for transfers between devices, steps(): from_below = lax.ppermute(far_share, AXES, up)  10.2 us
    pallas_call x2, Pallas kernels, far_call(): pl.pallas_call(functools.partial(above_kernel if last else below_kernel,...  6.55 us
    all_to_all x1, waiting for transfers between devices, steps(): mixed = lax.all_to_all(mixed, 'tm', split_axis=0, concat_axis=0, tiled=True)  5.13 us
    ppermute x1, starting transfers between devices, steps(): other = lax.ppermute(mine, 'tm', twin)  4.6 us
    ppermute x1, starting transfers between devices, steps(): source_a = lax.ppermute(own_share, AXES, even)  4.22 us
  transfers between devices with their start and end apart: 6, of which 2 were waited for; matrix products, arithmetic and copies ran while one was open for 0% of the time, Pallas kernels for 20%

profile of v3, /device:TPU:1, one launch (start us, length us, event | category | flops | bytes accessed | tf_op | source)
XLA Modules:
  0.0 92.0 jit_solution(3086118987259186421)
XLA Ops:
  0.0 0.0 copy-start.1
  0.0 0.0 copy-start.2
  0.0 0.0 copy-start
  0.0 3.3 %shard_map.64 = (bf16[4,2,128,384]{3,2,1,0:T(8,128)(2,1)}, bf16[20,128,128]{2,1,0:T(8,128)(2,1)}, bf16[16,128,128]{2,1,0:T(8,128)(2,1)}) custom-call(s32[4,8]{1,0:T(4,128)} %bitcast.12, bf16[128,128,128]{2,1,0:T(8,128)(2,1)} %integrals.3, bf16[128,384]{1,0:T(8,128)(2,1)} %bitcast.18, bf16[128,384]{1,0:T(8,128)(2,1)} %bitcast.19, bf16[128,512]{1,0:T(8,128)(2,1)} %coulomb.1), custom_call_target="tpu_custom_call" | custom-call | tf_op jit(solution)/shard_map/pallas_call | solution.py:78
  3.4 23.8 %all_to_all.10.mine = bf16[4,2,128,384]{3,2,1,0:T(8,128)(2,1)S(1)} all-to-all(bf16[4,2,128,384]{3,2,1,0:T(8,128)(2,1)} %get-tuple-element.11), channel_id=1, replica_groups={{0,2,4,6},{1,3,5,7},{8,10,12,14},{9,11,13,15},{16,18,20,22},{17,19,21,2..., dimensions={0} | all-to-all | bytes 1572864 | tf_op jit(solution)/shard_map/all_to_all | solution.py:320
  27.1 4.6 %collective-permute-start.1 = (bf16[4,2,128,384]{3,2,1,0:T(8,128)(2,1)S(1)}, bf16[4,2,128,384]{3,2,1,0:T(8,128)(2,1)S(1)}, u32[]{:S(2)}, u32[]{:S(2)}) collective-permute-start(bf16[4,2,128,384]{3,2,1,0:T(8,128)(2,1)S(1)} %all_to_all.10.mine), channel_id=1, source_target_pairs={{0,1},{1,0},{2,3},{3,2},{4,5},{5,4},{6,7},{7,6},{8,9},{9,8},{10,11... | collective-permute-start | bytes 2359304 | tf_op jit(solution)/shard_map/ppermute | solution.py:325
  31.7 4.2 %collective-permute-start.2 = (bf16[20,128,128]{2,1,0:T(8,128)(2,1)}, bf16[20,128,128]{2,1,0:T(8,128)(2,1)S(1)}, u32[]{:S(2)}, u32[]{:S(2)}) collective-permute-start(bf16[20,128,128]{2,1,0:T(8,128)(2,1)} %get-tuple-element.12), channel_id=1, source_target_pairs={{0,8},{1,9},{2,10},{3,11},{4,12},{5,13},{6,14},{7,15},{16,24},{17,... | collective-permute-start | bytes 1966088 | tf_op jit(solution)/shard_map/ppermute | solution.py:321
  36.0 1.3 %collective-permute-start.3 = (bf16[16,128,128]{2,1,0:T(8,128)(2,1)}, bf16[16,128,128]{2,1,0:T(8,128)(2,1)S(1)}, u32[]{:S(2)}, u32[]{:S(2)}) collective-permute-start(bf16[16,128,128]{2,1,0:T(8,128)(2,1)} %get-tuple-element.10), channel_id=1, source_target_pairs={{8,16},{9,17},{10,18},{11,19},{12,20},{13,21},{14,22},{15,23},{24,... | collective-permute-start | bytes 1572872 | tf_op jit(solution)/shard_map/ppermute | solution.py:319
  37.3 13.4 %collective-permute-start = (bf16[16,128,128]{2,1,0:T(8,128)(2,1)}, bf16[16,128,128]{2,1,0:T(8,128)(2,1)S(1)}, u32[]{:S(2)}, u32[]{:S(2)}) collective-permute-start(bf16[16,128,128]{2,1,0:T(8,128)(2,1)} %get-tuple-element.10), channel_id=1, source_target_pairs={{0,510},{1,511},{2,508},{3,509},{4,506},{5,507},{6,504},{7,505},{1... | collective-permute-start | bytes 1572872 | tf_op jit(solution)/shard_map/ppermute | solution.py:322
  50.7 0.0 copy-done.2
  50.7 1.9 %collective-permute-start.4 = (bf16[128,512]{1,0:T(8,128)(2,1)S(1)}, bf16[128,512]{1,0:T(8,128)(2,1)S(1)}, u32[]{:S(2)}, u32[]{:S(2)}) collective-permute-start(bf16[128,512]{1,0:T(8,128)(2,1)S(1)} %copy-done.2), channel_id=1, source_target_pairs={{8,16},{9,17},{10,18},{11,19},{12,20},{13,21},{14,22},{15,23},{24,... | collective-permute-start | bytes 393224 | tf_op jit(solution)/shard_map/ppermute | solution.py:323
  52.7 0.0 collective-permute-done.2.beside
  52.7 0.0 collective-permute-done.1.other
  52.7 0.0 copy-done.1
  52.7 0.0 copy-done
  52.7 12.2 %shard_map.65 = (f32[2,128,128]{2,1,0:T(8,128)S(1)}, bf16[128,16384]{1,0:T(8,128)(2,1)S(1)}) custom-call(bf16[20,128,128]{2,1,0:T(8,128)(2,1)S(1)} %collective-permute-done.2.beside, bf16[4,2,128,384]{3,2,1,0:T(8,128)(2,1)S(1)} %all_to_all.10.mine, bf16[4,2,128,384]{3,2,1,0:T(8,128)(2,1)S(1)} %collective-permute-done.1.other, ...), custom_call_target="tpu_custom_call" | custom-call | tf_op jit(solution)/shard_map/pallas_call | solution.py:254
  64.9 10.2 %collective-permute-done.3.source = bf16[16,128,128]{2,1,0:T(8,128)(2,1)S(1)} collective-permute-done((bf16[16,128,128]{2,1,0:T(8,128)(2,1)}, bf16[16,128,128]{2,1,0:T(8,128)(2,1)S(1)}, u32[]{:S(2)}, u32[]{:S(2)}) %collective-permute-start.3) | collective-permute-done | bytes 524320 | tf_op jit(solution)/shard_map/ppermute | solution.py:319
  75.1 5.2 %shard_map.66.below = f32[128,128]{1,0:T(8,128)S(1)} custom-call(bf16[16,128,128]{2,1,0:T(8,128)(2,1)S(1)} %collective-permute-done.3.source, bf16[4,2,128,384]{3,2,1,0:T(8,128)(2,1)S(1)} %all_to_all.10.mine, bf16[4,2,128,384]{3,2,1,0:T(8,128)(2,1)S(1)} %collective-permute-done.1.other, bf16[128,16384]{1,0:T(8,128)(2,1)S(1)} %get-tuple-element.13.own, ...), custom_call_target="tpu_custom_call" | custom-call | tf_op jit(solution)/shard_map/pallas_call | solution.py:279
  80.3 0.0 collective-permute-done.source
  80.3 1.3 %shard_map.67 = bf16[8,48,128]{2,1,0:T(8,128)(2,1)} custom-call(bf16[16,128,128]{2,1,0:T(8,128)(2,1)S(1)} %collective-permute-done.source, bf16[4,2,128,384]{3,2,1,0:T(8,128)(2,1)S(1)} %all_to_all.10.mine, bf16[4,2,128,384]{3,2,1,0:T(8,128)(2,1)S(1)} %collective-permute-done.1.other, bf16[128,16384]{1,0:T(8,128)(2,1)S(1)} %get-tuple-element.13.own, ...), custom_call_target="tpu_custom_call" | custom-call | tf_op jit(solution)/shard_map/pallas_call | solution.py:279
  81.6 4.1 %all-to-all-start.1 = ((bf16[8,48,128]{2,1,0:T(8,128)(2,1)}), bf16[8,48,128]{2,1,0:T(8,128)(2,1)S(1)}, u32[]{:S(2)}, u32[]{:S(2)}) async-start(bf16[8,48,128]{2,1,0:T(8,128)(2,1)} %shard_map.67), calls=%async_computation.1 | async-start | bytes 196608 | tf_op jit(solution)/shard_map/all_to_all | solution.py:329
  85.8 0.1 copy.7
  85.9 0.1 reshape_reshape.3
  85.9 0.0 collective-permute-done.4
  86.0 5.1 %all-to-all-done.1 = bf16[8,48,128]{2,1,0:T(8,128)(2,1)S(1)} async-done(((bf16[8,48,128]{2,1,0:T(8,128)(2,1)}), bf16[8,48,128]{2,1,0:T(8,128)(2,1)S(1)}, u32[]{:S(2)}, u32[]{:S(2)}) %all-to-all-start.1) | async-done | bytes 98336 | tf_op jit(solution)/shard_map/all_to_all | solution.py:329
  91.1 0.9 %convolution_bitcast_fusion = f32[1,128,512]{2,1,0:T(8,128)} fusion(bf16[8,48,128]{2,1,0:T(8,128)(2,1)S(1)} %all-to-all-done.1, bf16[8,48,512]{2,1,0:T(8,128)(2,1)S(1)} %pad_maximum_fusion), kind=kOutput, calls=%fused_computation | convolution fusion | flops 50331648 | bytes 753664 | tf_op jit(solution)/shard_map/dot_general | solution.py:334
  (2 shorter events, 0.0 us)
Async XLA Ops:
  0.0 52.7 %copy-start.1 = (s32[8,4]{0,1:T(4,128)S(1)}, s32[8,4]{0,1:T(4,128)}, u32[]{:S(2)}) copy-start(s32[8,4]{0,1:T(4,128)} %param.7) | copy-start | bytes 388
  0.0 50.7 %copy-start.2 = (bf16[128,512]{1,0:T(8,128)(2,1)S(1)}, bf16[128,512]{1,0:T(8,128)(2,1)}, u32[]{:S(2)}) copy-start(bf16[128,512]{1,0:T(8,128)(2,1)} %coulomb.1) | copy-start | bytes 393220
  0.0 52.7 %copy-start = (f32[8,8]{1,0:T(8,128)S(1)}, f32[8,8]{1,0:T(8,128)}, u32[]{:S(2)}) copy-start(f32[8,8]{1,0:T(8,128)} %cosine.5) | copy-start | bytes 772
  27.1 25.5 %collective-permute-start.1 = (bf16[4,2,128,384]{3,2,1,0:T(8,128)(2,1)S(1)}, bf16[4,2,128,384]{3,2,1,0:T(8,128)(2,1)S(1)}, u32[]{:S(2)}, u32[]{:S(2)}) collective-permute-start(bf16[4,2,128,384]{3,2,1,0:T(8,128)(2,1)S(1)} %all_to_all.10.mine), channel_id=1, source_target_pairs={{0,1},{1,0},{2,3},{3,2},{4,5},{5,4},{6,7},{7,6},{8,9},{9,8},{10,11... | collective-permute-start | bytes 2359304 | tf_op jit(solution)/shard_map/ppermute | solution.py:325
  31.7 20.9 %collective-permute-start.2 = (bf16[20,128,128]{2,1,0:T(8,128)(2,1)}, bf16[20,128,128]{2,1,0:T(8,128)(2,1)S(1)}, u32[]{:S(2)}, u32[]{:S(2)}) collective-permute-start(bf16[20,128,128]{2,1,0:T(8,128)(2,1)} %get-tuple-element.12), channel_id=1, source_target_pairs={{0,8},{1,9},{2,10},{3,11},{4,12},{5,13},{6,14},{7,15},{16,24},{17,... | collective-permute-start | bytes 1966088 | tf_op jit(solution)/shard_map/ppermute | solution.py:321
  36.0 39.1 %collective-permute-start.3 = (bf16[16,128,128]{2,1,0:T(8,128)(2,1)}, bf16[16,128,128]{2,1,0:T(8,128)(2,1)S(1)}, u32[]{:S(2)}, u32[]{:S(2)}) collective-permute-start(bf16[16,128,128]{2,1,0:T(8,128)(2,1)} %get-tuple-element.10), channel_id=1, source_target_pairs={{8,16},{9,17},{10,18},{11,19},{12,20},{13,21},{14,22},{15,23},{24,... | collective-permute-start | bytes 1572872 | tf_op jit(solution)/shard_map/ppermute | solution.py:319
  37.3 43.0 %collective-permute-start = (bf16[16,128,128]{2,1,0:T(8,128)(2,1)}, bf16[16,128,128]{2,1,0:T(8,128)(2,1)S(1)}, u32[]{:S(2)}, u32[]{:S(2)}) collective-permute-start(bf16[16,128,128]{2,1,0:T(8,128)(2,1)} %get-tuple-element.10), channel_id=1, source_target_pairs={{0,510},{1,511},{2,508},{3,509},{4,506},{5,507},{6,504},{7,505},{1... | collective-permute-start | bytes 1572872 | tf_op jit(solution)/shard_map/ppermute | solution.py:322
  50.7 35.2 %collective-permute-start.4 = (bf16[128,512]{1,0:T(8,128)(2,1)S(1)}, bf16[128,512]{1,0:T(8,128)(2,1)S(1)}, u32[]{:S(2)}, u32[]{:S(2)}) collective-permute-start(bf16[128,512]{1,0:T(8,128)(2,1)S(1)} %copy-done.2), channel_id=1, source_target_pairs={{8,16},{9,17},{10,18},{11,19},{12,20},{13,21},{14,22},{15,23},{24,... | collective-permute-start | bytes 393224 | tf_op jit(solution)/shard_map/ppermute | solution.py:323
  81.6 9.5 %all-to-all-start.1 = ((bf16[8,48,128]{2,1,0:T(8,128)(2,1)}), bf16[8,48,128]{2,1,0:T(8,128)(2,1)S(1)}, u32[]{:S(2)}, u32[]{:S(2)}) async-start(bf16[8,48,128]{2,1,0:T(8,128)(2,1)} %shard_map.67), calls=%async_computation.1 | async-start | bytes 196608 | tf_op jit(solution)/shard_map/all_to_all | solution.py:329
